TPU v7x, 8 devices: a whole 2x2x1 slice. The times are simulated.
8 devices in a mesh: layer: 1 (over z), tensor: 8 (over y, x, core).
Axes of the slice: x: 2, y: 2, z: 1, core: 2. Of those that a mesh axis runs over, the one named last changes fastest.
Arguments:
- gradient: bfloat16 [1024, 8192], P('layer', 'tensor')
- left_stat: float32 [1024, 1024], P('layer')
- right_stat: float32 [8192, 8192], P(('layer', 'tensor'))
- left_root: bfloat16 [1024, 1024], P('layer')
- right_root: bfloat16 [8192, 8192], P(('layer', 'tensor'))
- second_moment: float32 [1024, 8192], P('layer', 'tensor')
Outputs:
- output 1: float32 [1024, 1024], P('layer')
- output 2: float32 [8192, 8192], P(('layer', 'tensor'))
- output 3: float32 [1024, 8192], P('layer', 'tensor')
- output 4: float32 [1024, 8192], P('layer', 'tensor')
All inputs are finite; a program needn't handle non-finite values.
Results may differ from a plain program's by a relative error of at most 0.001.
Values are sent between devices in bfloat16 or wider.
A program may use at most 1 GiB of HBM per device.

v0:
```python
import jax
import jax.numpy as jnp
from jax import lax
from jax.sharding import PartitionSpec as P

EMA_DECAY = 0.9
ADAM_EPS = 1e-8


def solution(mesh):
    col_spec = P('layer', 'tensor')
    rep_spec = P('layer', None)
    row_spec = P(('layer', 'tensor'), None)

    def local_step(grad_loc, left_stat, right_loc, left_root, root_loc, moment_loc):
        grad_full = lax.all_gather(grad_loc, 'tensor', axis=1, tiled=True)
        left_part = lax.dot_general(grad_loc, grad_loc, (((1,), (1,)), ((), ())), preferred_element_type=jnp.float32)
        left_sum = lax.psum(left_part, 'tensor')
        left_new = EMA_DECAY * left_stat + (1.0 - EMA_DECAY) * left_sum
        right_prod = lax.dot_general(grad_loc, grad_full, (((0,), (0,)), ((), ())), preferred_element_type=jnp.float32)
        right_new = EMA_DECAY * right_loc + (1.0 - EMA_DECAY) * right_prod
        precond = lax.dot_general(grad_full, root_loc, (((1,), (1,)), ((), ())), preferred_element_type=jnp.float32).astype(jnp.bfloat16)
        direction = jnp.dot(left_root, precond, preferred_element_type=jnp.float32)
        grad_f32 = grad_loc.astype(jnp.float32)
        moment_new = EMA_DECAY * moment_loc + (1.0 - EMA_DECAY) * grad_f32 * grad_f32
        adam_dir = grad_f32 / (jnp.sqrt(moment_new) + ADAM_EPS)
        local_sq = jnp.stack([jnp.sum(adam_dir * adam_dir), jnp.sum(direction * direction)])
        total_sq = lax.psum(local_sq, 'tensor')
        return (left_new, right_new, direction * jnp.sqrt(total_sq[0] / total_sq[1]), moment_new)

    return jax.shard_map(local_step, mesh=mesh, in_specs=(col_spec, rep_spec, row_spec, rep_spec, row_spec, col_spec), out_specs=(rep_spec, row_spec, col_spec, col_spec), check_vma=False)
```

profile of v0, /device:TPU:0, one launch (start us, length us, event | category | flops | bytes accessed | tf_op | source)
XLA Modules:
  0.0 256.7 jit_solution(14788019211639170824)
XLA Ops:
  7.2 0.0 copy-start
  7.2 0.0 all-gather.2.cloned.1.call-start
  7.2 0.7 all-gather.2.cloned.1.call-update
  7.9 0.0 all-reduce.2.cloned.1.call-start
  8.0 6.6 %fusion.7 = f32[1024,1024]{1,0:T(8,128)} fusion(bf16[1024,1024]{1,0:T(8,128)(2,1)} %param.6), kind=kOutput, calls=%fused_computation.13 | convolution fusion | flops 2147483648 | bytes 6291456 | tf_op jit(solution)/shard_map/dot_general | solution.py:17
  14.6 0.0 all-reduce.2.cloned.1.call-update
  14.6 7.8 %fusion.2 = (f32[]{:T(128)}, f32[1024,1024]{1,0:T(8,128)}) fusion(bf16[1024,1024]{1,0:T(8,128)(2,1)} %param.6, f32[1024,1024]{1,0:T(8,128)} %param.11), kind=kLoop, calls=%fused_computation.8 | loop fusion | flops 9437183 | bytes 10485764 | tf_op jit(solution)/shard_map/reduce_sum | solution.py:27
  22.4 74.4 %all-gather.2.cloned.1.call-done = bf16[1024,8192]{1,0:T(8,128)(2,1)} async-done(((bf16[1024,1024]{1,0:T(8,128)(2,1)}), bf16[1024,8192]{1,0:T(8,128)(2,1)}) %all-gather.2.cloned.1.call-update) | async-done | bytes 16777232 | tf_op jit(solution)/shard_map/all_gather | solution.py:16
  96.8 22.1 %fusion.8 = bf16[1024,1024]{1,0:T(8,128)(2,1)S(1)} fusion(bf16[1024,8192]{1,0:T(8,128)(2,1)} %all-gather.2.cloned.1.call-done, bf16[1024,8192]{1,0:T(8,128)(2,1)} %param.10), kind=kOutput, calls=%fused_computation.14 | convolution fusion | flops 17179869184 | bytes 35651584 | tf_op jit(solution)/shard_map/dot_general | solution.py:22
  118.8 0.0 copy-done
  118.8 5.2 %multiply_reduce_fusion = (f32[]{:T(128)}, f32[1024,1024]{1,0:T(8,128)}) fusion(bf16[1024,1024]{1,0:T(8,128)(2,1)S(1)} %fusion.8, bf16[1024,1024]{1,0:T(8,128)(2,1)S(1)} %copy-done), kind=kOutput, calls=%fused_computation.6 | convolution fusion | flops 2149580800 | bytes 8388612 | tf_op jit(solution)/shard_map/dot_general | solution.py:23
  124.0 1.3 pad_maximum_fusion
  125.3 44.6 %all-reduce.2.cloned.1.call-done = f32[1024,1024]{1,0:T(8,128)} async-done(((f32[1024,1024]{1,0:T(8,128)}), f32[1024,1024]{1,0:T(8,128)}) %all-reduce.2.cloned.1.call-update) | async-done | bytes 4194320 | tf_op jit(solution)/shard_map/psum | solution.py:18
  169.9 7.0 %multiply_add_fusion.1 = f32[1024,1024]{1,0:T(8,128)} fusion(f32[1024,1024]{1,0:T(8,128)} %all-reduce.2.cloned.1.call-done, f32[1024,1024]{1,0:T(8,128)} %param.7), kind=kLoop, calls=%fused_computation.7 | loop fusion | flops 3145728 | bytes 12582912 | tf_op jit(solution)/shard_map/add | solution.py:19
  176.9 22.5 %psum.15 = f32[2]{0:T(128)S(1)} all-reduce(f32[2]{0:T(128)S(1)} %pad_maximum_fusion), channel_id=1, replica_groups=mesh['layer'=1,'tensor'=8] {'tensor'}, use_global_device_ids=true, to_apply=%region_3.0 | all-reduce | flops 2 | bytes 16 | tf_op jit(solution)/shard_map/psum | solution.py:28
  199.4 0.6 fusion.6
  201.2 5.0 %multiply_bitcast_fusion = f32[1024,1024]{0,1:T(8,128)} fusion(f32[1024,1024]{1,0:T(8,128)} %get-tuple-element.13, f32[]{:T(128)} %bitcast.2), kind=kLoop, calls=%fused_computation.5 | loop fusion | flops 1048576 | bytes 8388612 | tf_op jit(solution)/shard_map/mul | solution.py:29
  206.3 5.3 %copy.10 = f32[1024,1024]{1,0:T(8,128)} copy(f32[1024,1024]{0,1:T(8,128)} %multiply_bitcast_fusion) | data formatting | bytes 8388608
  211.6 0.0 copy-start.1
  211.6 38.2 %multiply_add_fusion = f32[1024,8192]{1,0:T(8,128)} fusion(f32[1024,8192]{1,0:T(8,128)} %param.8, bf16[1024,1024]{1,0:T(8,128)(2,1)} %param.6, bf16[1024,8192]{1,0:T(8,128)(2,1)} %all-gather.2.cloned.1.call-done), kind=kOutput, calls=%fused_computation | convolution fusion | flops 17205035008 | bytes 85983232 | tf_op jit(solution)/shard_map/dot_general | solution.py:20
  249.8 0.0 copy-done.1
Async XLA Ops:
  7.2 111.7 %copy-start = (bf16[1024,1024]{1,0:T(8,128)(2,1)S(1)}, bf16[1024,1024]{1,0:T(8,128)(2,1)}, u32[]{:S(2)}) copy-start(bf16[1024,1024]{1,0:T(8,128)(2,1)} %param.9) | copy-start | bytes 6291460
  7.2 89.6 %all-gather.2.cloned.1.call-start = ((), (), s32[]{:S(2)}) async-start(), calls=%async_computation.1 | async-start | bytes 18874368 | tf_op jit(solution)/shard_map/all_gather | solution.py:16
  7.9 162.0 %all-reduce.2.cloned.1.call-start = ((), (), s32[]{:S(2)}) async-start(), calls=%async_computation | async-start | bytes 8388608 | tf_op jit(solution)/shard_map/psum | solution.py:18
  211.6 38.2 %copy-start.1 = (bf16[1024,1024]{1,0:T(8,128)(2,1)S(1)}, bf16[1024,1024]{1,0:T(8,128)(2,1)}, u32[]{:S(2)}) copy-start(bf16[1024,1024]{1,0:T(8,128)(2,1)} %param.9) | copy-start | bytes 6291460
Sparse Core Ops, SparseCore 0:
  9.8 86.8 all-gather.1
  100.6 69.2 all-reduce.1
where the time goes:
time: 257 us
  waiting for transfers between devices  120 us (47%)
  matrix products  72 us (28%)
  blocking collectives  22.5 us (9%)
  other arithmetic  21.1 us (8%)
  between operations  15.4 us (6%)
  local copies, waits for them, and re-layouts  5.94 us (2%)
    all_gather x1, waiting for transfers between devices, local_step(): grad_full = lax.all_gather(grad_loc, 'tensor', axis=1, tiled=True)  74.4 us
    psum x1, waiting for transfers between devices, local_step(): left_sum = lax.psum(left_part, 'tensor')  44.6 us
    dot_general x1, matrix products, local_step(): lax.dot_general(grad_loc, grad_full, (((0,), (0,)), ((), ())), preferred_...  38.2 us
    psum x1, blocking collectives, local_step(): total_sq = lax.psum(local_sq, 'tensor')  22.5 us
    dot_general x1, matrix products, local_step(): lax.dot_general(grad_full, root_loc, (((1,), (1,)), ((), ())), preferred_...  22.1 us
    reduce_sum x1, other arithmetic, local_step(): jnp.sum(adam_dir * adam_dir)  7.76 us
    add x1, other arithmetic, local_step(): left_new = EMA_DECAY * left_stat + (1.0 - EMA_DECAY) * left_sum  6.97 us
    dot_general x1, matrix products, local_step(): lax.dot_general(grad_loc, grad_loc, (((1,), (1,)), ((), ())), preferred_e...  6.61 us
  transfers between devices with their start and end apart: 2, of which 2 were waited for; matrix products, arithmetic and copies ran while one was open for 17% of the time, Pallas kernels for 0%

commit v1 on v0

--- a/solution.py
+++ b/solution.py
@@ -14,8 +14,13 @@
 
     def local_step(grad_loc, left_stat, right_loc, left_root, root_loc, moment_loc):
         grad_full = lax.all_gather(grad_loc, 'tensor', axis=1, tiled=True)
-        left_part = lax.dot_general(grad_loc, grad_loc, (((1,), (1,)), ((), ())), preferred_element_type=jnp.float32)
-        left_sum = lax.psum(left_part, 'tensor')
+        me = lax.axis_index('tensor')
+        width = grad_loc.shape[1]
+        left_sum = lax.dot_general(grad_loc, grad_loc, (((1,), (1,)), ((), ())), preferred_element_type=jnp.float32)
+        for hop in range(1, 8):
+            other = lax.rem(me + hop, 8)
+            block = lax.dynamic_slice_in_dim(grad_full, other * width, width, 1)
+            left_sum = left_sum + lax.dot_general(block, block, (((1,), (1,)), ((), ())), preferred_element_type=jnp.float32)
         left_new = EMA_DECAY * left_stat + (1.0 - EMA_DECAY) * left_sum
         right_prod = lax.dot_general(grad_loc, grad_full, (((0,), (0,)), ((), ())), preferred_element_type=jnp.float32)
         right_new = EMA_DECAY * right_loc + (1.0 - EMA_DECAY) * right_prod

time: 257 us -> 254 us (0.988)
  matrix products: 72 us -> 114 us
  waiting for transfers between devices: 120 us -> 81.8 us
  other arithmetic: 21.1 us -> 14.1 us
    psum x1 -> x0, waiting for transfers between devices: 44.6 us -> none  [local_step(): left_sum = lax.psum(left_part, 'tensor')]
    dot_general x0 -> x7, matrix products: none -> 35.5 us  [local_step(): lax.dot_general(block, block, (((1,), (1,)), ((), ())), preferred_element...]
    add x1 -> x0, other arithmetic: 6.97 us -> none  [local_step(): left_new = EMA_DECAY * left_stat + (1.0 - EMA_DECAY) * left_sum]
    dot_general x1, matrix products: 6.61 us -> 13.5 us  [local_step(): lax.dot_general(grad_loc, grad_loc, (((1,), (1,)), ((), ())), preferred_e...]
    all_gather x1, waiting for transfers between devices: 74.4 us -> 81.1 us  [local_step(): grad_full = lax.all_gather(grad_loc, 'tensor', axis=1, tiled=True)]
    unnamed x5 -> x17, local copies, waits for them, and re-layouts: 5.35 us -> 5.38 us
  transfers between devices with their start and end apart: 2 -> 1, of which waited for: 2 -> 1; matrix products, arithmetic and copies ran while one was open for 17% -> 3% of each run, Pallas kernels for 0% -> 0%
where the time goes in v1:
time: 254 us
  matrix products  114 us (45%)
  waiting for transfers between devices  81.8 us (32%)
  blocking collectives  22.2 us (9%)
  between operations  15.5 us (6%)
  other arithmetic  14.1 us (6%)
  local copies, waits for them, and re-layouts  5.96 us (2%)
    all_gather x1, waiting for transfers between devices, local_step(): grad_full = lax.all_gather(grad_loc, 'tensor', axis=1, tiled=True)  81.1 us
    dot_general x1, matrix products, local_step(): lax.dot_general(grad_loc, grad_full, (((0,), (0,)), ((), ())), preferred_...  38.2 us
    dot_general x7, matrix products, local_step(): lax.dot_general(block, block, (((1,), (1,)), ((), ())), preferred_element...  35.5 us
    psum x1, blocking collectives, local_step(): total_sq = lax.psum(local_sq, 'tensor')  22.2 us
    dot_general x1, matrix products, local_step(): lax.dot_general(grad_full, root_loc, (((1,), (1,)), ((), ())), preferred_...  22.1 us
    dot_general x1, matrix products, local_step(): lax.dot_general(grad_loc, grad_loc, (((1,), (1,)), ((), ())), preferred_e...  13.5 us
    reduce_sum x1, other arithmetic, local_step(): jnp.sum(adam_dir * adam_dir)  7.72 us
    unnamed x17, local copies, waits for them, and re-layouts  5.38 us
  transfers between devices with their start and end apart: 1, of which 1 were waited for; matrix products, arithmetic and copies ran while one was open for 3% of the time, Pallas kernels for 0%

profile of v1, /device:TPU:0, one launch (start us, length us, event | category | flops | bytes accessed | tf_op | source)
XLA Modules:
  0.0 254.0 jit_solution(1660957801195745321)
XLA Ops:
  7.2 0.0 copy-start
  7.2 0.0 all-gather.2.cloned.1.call-start
  7.2 0.7 all-gather.2.cloned.1.call-update
  8.0 7.7 %fusion.2 = (f32[]{:T(128)}, f32[1024,1024]{1,0:T(8,128)}) fusion(bf16[1024,1024]{1,0:T(8,128)(2,1)} %param.6, f32[1024,1024]{1,0:T(8,128)} %param.11), kind=kLoop, calls=%fused_computation.8 | loop fusion | flops 9437183 | bytes 10485764 | tf_op jit(solution)/shard_map/reduce_sum | solution.py:32
  15.7 81.1 %all-gather.2.cloned.1.call-done = bf16[1024,8192]{1,0:T(8,128)(2,1)} async-done(((bf16[1024,1024]{1,0:T(8,128)(2,1)}), bf16[1024,8192]{1,0:T(8,128)(2,1)}) %all-gather.2.cloned.1.call-update) | async-done | bytes 16777232 | tf_op jit(solution)/shard_map/all_gather | solution.py:16
  96.8 22.1 %fusion.28 = bf16[1024,1024]{1,0:T(8,128)(2,1)S(1)} fusion(bf16[1024,8192]{1,0:T(8,128)(2,1)} %all-gather.2.cloned.1.call-done, bf16[1024,8192]{1,0:T(8,128)(2,1)} %param.10), kind=kOutput, calls=%fused_computation.34 | convolution fusion | flops 17179869184 | bytes 35651584 | tf_op jit(solution)/shard_map/dot_general | solution.py:27
  118.8 0.0 copy-done
  118.8 5.2 %multiply_reduce_fusion = (f32[]{:T(128)}, f32[1024,1024]{1,0:T(8,128)}) fusion(bf16[1024,1024]{1,0:T(8,128)(2,1)S(1)} %fusion.28, bf16[1024,1024]{1,0:T(8,128)(2,1)S(1)} %copy-done), kind=kOutput, calls=%fused_computation.6 | convolution fusion | flops 2149580800 | bytes 8388612 | tf_op jit(solution)/shard_map/dot_general | solution.py:28
  124.0 1.4 pad_maximum_fusion
  125.4 22.2 %psum.7 = f32[2]{0:T(128)S(1)} all-reduce(f32[2]{0:T(128)S(1)} %pad_maximum_fusion), channel_id=1, replica_groups=mesh['layer'=1,'tensor'=8] {'tensor'}, use_global_device_ids=true, to_apply=%region_2.0 | all-reduce | flops 2 | bytes 16 | tf_op jit(solution)/shard_map/psum | solution.py:33
  147.6 0.6 fusion.27
  149.5 5.0 %multiply_bitcast_fusion = f32[1024,1024]{0,1:T(8,128)} fusion(f32[1024,1024]{1,0:T(8,128)} %get-tuple-element.13, f32[]{:T(128)} %bitcast.2), kind=kLoop, calls=%fused_computation.5 | loop fusion | flops 1048576 | bytes 8388612 | tf_op jit(solution)/shard_map/mul | solution.py:34
  154.6 5.3 %copy.10 = f32[1024,1024]{1,0:T(8,128)} copy(f32[1024,1024]{0,1:T(8,128)} %multiply_bitcast_fusion) | data formatting | bytes 8388608
  159.9 0.0 slice-start
  159.9 0.0 slice-start.1
  159.9 6.8 %fusion.5 = f32[1024,1024]{1,0:T(8,128)} fusion(bf16[1024,8192]{1,0:T(8,128)(2,1)} %all-gather.2.cloned.1.call-done, s32[]{:T(128)S(6)} %select_n.27), kind=kOutput, calls=%fused_computation.11 | convolution fusion | flops 2147483648 | bytes 6291460 | tf_op jit(solution)/shard_map/dot_general | solution.py:23
  166.7 0.0 slice-start.2
  166.7 0.0 slice-start.3
  166.7 6.8 %fusion.7 = f32[1024,1024]{1,0:T(8,128)} fusion(bf16[1024,8192]{1,0:T(8,128)(2,1)} %all-gather.2.cloned.1.call-done, s32[]{:T(128)S(6)} %select_n.26), kind=kOutput, calls=%fused_computation.13 | convolution fusion | flops 2147483648 | bytes 6291460 | tf_op jit(solution)/shard_map/dot_general | solution.py:23
  173.4 0.0 slice-done
  173.4 0.0 slice-done.1
  173.4 0.0 slice-done.2
  173.4 0.0 slice-done.3
  173.5 4.3 %fusion.9 = f32[1024,1024]{1,0:T(8,128)} fusion(bf16[1024,8192]{1,0:T(8,128)(2,1)S(1)} %bitcast.14, s32[]{:T(128)S(6)} %select_n.25), kind=kOutput, calls=%fused_computation.15 | convolution fusion | flops 2147483648 | bytes 6291460 | tf_op jit(solution)/shard_map/dot_general | solution.py:23
  177.8 4.3 %fusion.11 = f32[1024,1024]{1,0:T(8,128)} fusion(bf16[1024,8192]{1,0:T(8,128)(2,1)S(1)} %bitcast.14, s32[]{:T(128)S(6)} %select_n.24), kind=kOutput, calls=%fused_computation.17 | convolution fusion | flops 2147483648 | bytes 6291460 | tf_op jit(solution)/shard_map/dot_general | solution.py:23
  182.1 4.3 %fusion.13 = f32[1024,1024]{1,0:T(8,128)} fusion(bf16[1024,8192]{1,0:T(8,128)(2,1)S(1)} %bitcast.14, s32[]{:T(128)S(6)} %select_n.23), kind=kOutput, calls=%fused_computation.19 | convolution fusion | flops 2147483648 | bytes 6291460 | tf_op jit(solution)/shard_map/dot_general | solution.py:23
  186.5 4.3 %fusion.15 = f32[1024,1024]{1,0:T(8,128)} fusion(bf16[1024,8192]{1,0:T(8,128)(2,1)S(1)} %bitcast.14, s32[]{:T(128)S(6)} %select_n.22), kind=kOutput, calls=%fused_computation.21 | convolution fusion | flops 2147483648 | bytes 6291460 | tf_op jit(solution)/shard_map/dot_general | solution.py:23
  190.8 0.0 copy-start.2
  190.8 0.0 copy-start.3
  190.8 4.7 %fusion.17 = f32[1024,1024]{1,0:T(8,128)} fusion(bf16[1024,8192]{1,0:T(8,128)(2,1)S(1)} %bitcast.14, s32[]{:T(128)S(6)} %select_n.21), kind=kOutput, calls=%fused_computation.23 | convolution fusion | flops 2147483648 | bytes 6291460 | tf_op jit(solution)/shard_map/dot_general | solution.py:23
  195.4 0.0 copy-done.2
  195.4 0.0 copy-done.3
  195.4 13.5 %multiply_add_fusion.1 = f32[1024,1024]{1,0:T(8,128)} fusion(f32[1024,1024]{1,0:T(8,128)} %fusion.5, f32[1024,1024]{1,0:T(8,128)} %fusion.7, f32[1024,1024]{1,0:T(8,128)} %fusion.9, f32[1024,1024]{1,0:T(8,128)} %fusion.11, f32[1024,1024]{1,0:T(8,128)} %fusion.13, f32[1024,1024]{1,0:T(8,128)} %fusion.15, f32[1024,1024]{1,0:T(8,128)} %fusion.17, ...), kind=kOutput, calls=%fused_computation.7 | convolution fusion | flops 2157969408 | bytes 39845888 | tf_op jit(solution)/shard_map/dot_general | solution.py:19
  208.9 0.0 copy-start.1
  209.0 38.2 %multiply_add_fusion = f32[1024,8192]{1,0:T(8,128)} fusion(f32[1024,8192]{1,0:T(8,128)} %param.8, bf16[1024,1024]{1,0:T(8,128)(2,1)} %param.6, bf16[1024,8192]{1,0:T(8,128)(2,1)} %all-gather.2.cloned.1.call-done), kind=kOutput, calls=%fused_computation | convolution fusion | flops 17205035008 | bytes 85983232 | tf_op jit(solution)/shard_map/dot_general | solution.py:25
  247.2 0.0 copy-done.1
  (1 shorter events, 0.0 us)
Async XLA Ops:
  7.2 111.7 %copy-start = (bf16[1024,1024]{1,0:T(8,128)(2,1)S(1)}, bf16[1024,1024]{1,0:T(8,128)(2,1)}, u32[]{:S(2)}) copy-start(bf16[1024,1024]{1,0:T(8,128)(2,1)} %param.9) | copy-start | bytes 6291460
  7.2 89.6 %all-gather.2.cloned.1.call-start = ((), (), s32[]{:S(2)}) async-start(), calls=%async_computation | async-start | bytes 18874368 | tf_op jit(solution)/shard_map/all_gather | solution.py:16
  159.9 13.5 %slice-start = ((s8[16777216]{0:T(1024)(128)(4,1)}), s8[4194304]{0:T(1024)(128)(4,1)S(1)}, s32[]{:S(2)}) async-start(s8[16777216]{0:T(1024)(128)(4,1)} %bitcast.13), calls=%async_computation.1 | async-start | bytes 8388608
  159.9 13.5 %slice-start.1 = ((s8[16777216]{0:T(1024)(128)(4,1)}), s8[4194304]{0:T(1024)(128)(4,1)S(1)}, s32[]{:S(2)}) async-start(s8[16777216]{0:T(1024)(128)(4,1)} %bitcast.13), calls=%async_computation.2 | async-start | bytes 8388608
  166.7 6.8 %slice-start.2 = ((s8[16777216]{0:T(1024)(128)(4,1)}), s8[4194304]{0:T(1024)(128)(4,1)S(1)}, s32[]{:S(2)}) async-start(s8[16777216]{0:T(1024)(128)(4,1)} %bitcast.13), calls=%async_computation.3 | async-start | bytes 8388608
  166.7 6.8 %slice-start.3 = ((s8[16777216]{0:T(1024)(128)(4,1)}), s8[4194304]{0:T(1024)(128)(4,1)S(1)}, s32[]{:S(2)}) async-start(s8[16777216]{0:T(1024)(128)(4,1)} %bitcast.13), calls=%async_computation.4 | async-start | bytes 8388608
  190.8 4.7 %copy-start.2 = (bf16[1024,1024]{1,0:T(8,128)(2,1)S(1)}, bf16[1024,1024]{1,0:T(8,128)(2,1)}, u32[]{:S(2)}) copy-start(bf16[1024,1024]{1,0:T(8,128)(2,1)} %param.6) | copy-start | bytes 6291460
  190.8 4.7 %copy-start.3 = (f32[1024,1024]{1,0:T(8,128)S(1)}, f32[1024,1024]{1,0:T(8,128)}, u32[]{:S(2)}) copy-start(f32[1024,1024]{1,0:T(8,128)} %param.7) | copy-start | bytes 12582916
  208.9 38.2 %copy-start.1 = (bf16[1024,1024]{1,0:T(8,128)(2,1)S(1)}, bf16[1024,1024]{1,0:T(8,128)(2,1)}, u32[]{:S(2)}) copy-start(bf16[1024,1024]{1,0:T(8,128)(2,1)} %param.9) | copy-start | bytes 6291460
Sparse Core Ops, SparseCore 0:
  9.8 86.8 all-gather.1

commit v2 on v0

v2 whole, which is shorter than its diff:
```python
import jax
import jax.numpy as jnp
from jax import lax
from jax.experimental import pallas as pl
from jax.experimental.pallas import tpu as pltpu
from jax.sharding import PartitionSpec as P

EMA_DECAY = 0.9
ADAM_EPS = 1e-8
N = 1024
CW = 128
GW = 512
TW = 256
NDEV = 8
ICI = 12
EARLY = 4
F32 = jnp.float32
BF16 = jnp.bfloat16

NT = (((1,), (1,)), ((), ()))
NN = (((1,), (0,)), ((), ()))


def dot(a, b, dims):
    return lax.dot_general(a, b, dims, preferred_element_type=F32)


def gather_kernel(g_hbm, l_hbm, r_hbm, lr_hbm, rr_hbm, v_hbm,
                  r0, r1, r2, r3, r4, r5, r6, r7, dd, ln, ratio,
                  gg, gt, rr, mine, sums,
                  load_sem, rload_sem, rr_sem, lr_sem,
                  own_s, own_r, x_s, x_r, y_s, y_r, p_s, p_r, n_s, n_r):
    rn = (r0, r1, r2, r3, r4, r5, r6, r7)
    me = lax.axis_index('tensor')
    core = lax.rem(me, 2)
    xpos = lax.rem(lax.div(me, 2), 2)
    ypos = lax.div(me, 4)
    mate = me + 1 - 2 * core
    xnb = me + 2 - 4 * xpos
    ynb = me + 4 - 8 * ypos
    diag = xnb + 4 - 8 * ypos
    mx = mate + 2 - 4 * xpos
    my = mate + 4 - 8 * ypos
    md = mx + 4 - 8 * ypos

    def col(dev, chunk):
        return pl.multiple_of(dev * N + chunk * CW, CW)

    blocks = (me, mate, xnb, ynb, mx, my, diag, md)

    def group(g, late=False):
        if isinstance(g, int) and g < 4:
            return [(g // 2, (g % 2) * 4 + j) for j in range(4)]
        i = g - 4
        if late:
            return [(6, i - 8), (6, i - 4), (7, i - 8), (7, i - 4)]
        return [(2, lax.rem(i + 4, 8)), (3, i), (4, lax.rem(i + 4, 8)), (5, i)]

    def lanes(j, w=CW):
        return pl.ds(j * w, w)

    own_loads = [pltpu.make_async_copy(g_hbm.at[:, h * GW:(h + 1) * GW], gg.at[h], load_sem.at[h]) for h in range(2)]
    v_load = pltpu.make_async_copy(v_hbm, dd, load_sem.at[2])
    half = pl.ds(pl.multiple_of(core * GW, GW), GW)
    l_load = pltpu.make_async_copy(l_hbm.at[half, :], ln.at[half, :], load_sem.at[3])
    for c in own_loads:
        c.start()

    r_loads = [pltpu.make_async_copy(r_hbm.at[:, pl.ds(pl.multiple_of(dev * N, N), N)], rn[k], rload_sem.at[k])
               for k, dev in enumerate(blocks)]

    def rr_loads(pieces, slot):
        return [pltpu.make_async_copy(rr_hbm.at[:, pl.ds(col(blocks[b], c), CW)], rr.at[slot, :, lanes(j)], rr_sem.at[slot, j])
                for j, (b, c) in enumerate(pieces)]

    barrier = pltpu.get_barrier_semaphore()
    others = [lax.rem(me + k, NDEV) for k in range(1, NDEV)]
    for o in others:
        pl.semaphore_signal(barrier, inc=1, device_id={'tensor': o})
    v_load.start()
    for c in rr_loads(group(0), 0):
        c.start()
    r_loads[0].start()
    l_load.start()
    r_loads[1].start()
    for c in own_loads:
        c.wait()
    pl.semaphore_wait(barrier, NDEV - 1)

    def own_send(h):
        return pltpu.make_async_remote_copy(gg.at[h], gg.at[2 + h], own_s.at[h], own_r.at[h], device_id={'tensor': mate})

    def x_copy(n, src):
        return pltpu.make_async_remote_copy(src, gg.at[4 + n, :, lanes(0)], x_s.at[n], x_r.at[n], device_id={'tensor': xnb})

    def y_copy(n, src):
        return pltpu.make_async_remote_copy(src, gg.at[4 + n, :, lanes(1)], y_s.at[n], y_r.at[n], device_id={'tensor': ynb})

    def own_chunk(c):
        return gg.at[lax.div(c, 4), :, pl.ds(pl.multiple_of(lax.rem(c, 4) * CW, CW), CW)]

    def send_own(n):
        x_copy(n, own_chunk(lax.rem(n + 4, 8))).start()
        y_copy(n, own_chunk(n)).start()

    def send_forward(j):
        x_copy(8 + j, gg.at[4 + j, :, lanes(1)]).start()
        y_copy(8 + j, gg.at[4 + j, :, lanes(0)]).start()

    def mate_copy(i):
        return pltpu.make_async_remote_copy(gg.at[4 + i, :, lanes(0, TW)], gg.at[4 + i, :, lanes(1, TW)],
                                            p_s.at[i], p_r.at[i], device_id={'tensor': mate})

    for n in range(EARLY):
        send_own(jnp.int32(n))
    for h in range(2):
        own_send(h).start()
    for c in r_loads[2:]:
        c.start()

    v_load.wait()

    def adam(k, total):
        rows = pl.ds(pl.multiple_of(k * 64, 64), 64)
        for h in range(2):
            grad = gg[h, rows, :].astype(F32)
            moment = EMA_DECAY * dd[rows, lanes(h, GW)] + (1.0 - EMA_DECAY) * grad * grad
            a = grad / (jnp.sqrt(moment) + ADAM_EPS)
            total = total + jnp.sum(a * a, axis=0, keepdims=True)
        return total

    adam_sum = jnp.sum(lax.fori_loop(0, N // 64, adam, jnp.zeros((1, GW), F32)))

    def transpose(k, _):
        rows = pl.ds(pl.multiple_of(k * CW, CW), CW)
        for h in range(2):
            gt[lanes(h, GW), rows] = gg[h, rows, :].T
        return 0

    lax.fori_loop(0, N // CW, transpose, 0)

    def x_part(g, slot, first, k0, kw):
        def tile(n, _):
            cols = pl.ds(pl.multiple_of(n * TW, TW), TW)
            part = dot(gg[g, :, pl.ds(k0, kw)], rr[slot, cols, pl.ds(k0, kw)], NT)
            dd[:, cols] = part if first else dd[:, cols] + part
            return 0
        lax.fori_loop(0, N // TW, tile, 0)

    def r_part(g, h, pieces):
        part = (1.0 - EMA_DECAY) * dot(gt[...], gg[g, :, lanes(h, TW)], NN)
        for j in range(2):
            b, c = pieces[2 * h + j]
            where = pl.ds(pl.multiple_of(c * CW, CW), CW)
            rn[b][:, where] = EMA_DECAY * rn[b][:, where] + part[:, j * CW:(j + 1) * CW]

    def l_part(g, rows):
        def tile(n, _):
            cols = pl.ds(pl.multiple_of(n * TW, TW), TW)
            part = dot(gg[g, rows, :], gg[g, cols, :], NT)
            ln[rows, cols] = ln[rows, cols] + (1.0 - EMA_DECAY) * part
            return 0
        lax.fori_loop(0, N // TW, tile, 0)

    l_load.wait()

    def decay(k, _):
        rows = pl.ds(pl.multiple_of(core * GW + k * 64, 64), 64)
        ln[rows, :] = EMA_DECAY * ln[rows, :]
        return 0

    lax.fori_loop(0, GW // 64, decay, 0)

    for g in range(4):
        slot = g % 2
        for c in rr_loads(group(g + 1), 1 - slot):
            c.start()
        cols = group(g)
        if g == 2:
            own_send(0).wait()
            r_loads[1].wait()
        if g == 3:
            own_send(1).wait()
        if g == 0:
            r_loads[0].wait()
        for c in rr_loads(cols, slot):
            c.wait()
        x_part(g, slot, g == 0, 0, GW)
        for h in range(2):
            r_part(g, h, cols)
        l_part(g, half)
    for c in r_loads[2:]:
        c.wait()

    def arrive(i):
        x_copy(i, gg.at[4 + i, :, lanes(0)]).wait_recv()
        y_copy(i, gg.at[4 + i, :, lanes(1)]).wait_recv()
        mate_copy(i).start()

    def step(i, issue, late, next_late):
        g = 4 + i
        slot = lax.rem(i, 2)
        cols = group(g, late)
        for c in rr_loads(group(g + 1, next_late), 1 - slot):
            c.start()
        arrive(i)
        issue(i)
        r_part(g, 0, cols)
        mate_copy(i).wait_recv()
        r_part(g, 1, cols)
        for c in rr_loads(cols, slot):
            c.wait()
        x_part(g, slot, False, 0, GW)
        l_part(g, half)

    def first_steps(i, _):
        step(i, lambda n: send_own(n + 4), False, False)
        return 0

    def next_steps(i, _):
        step(i, lambda n: send_forward(n - 4), False, False)
        return 0

    def last_steps(i, _):
        step(i, lambda n: None, True, True)
        return 0

    lax.fori_loop(0, 4, first_steps, 0)
    lax.fori_loop(4, 7, next_steps, 0)
    step(jnp.int32(7), lambda n: send_forward(n - 4), False, True)

    for n in range(8):
        x_copy(n, own_chunk(jnp.int32((n + 4) % 8))).wait_send()
        y_copy(n, own_chunk(jnp.int32(n))).wait_send()
    lr_loads = [pltpu.make_async_copy(lr_hbm.at[:, h * GW:(h + 1) * GW], gg.at[h], lr_sem.at[h]) for h in range(2)]
    for c in lr_loads:
        c.start()
    lax.fori_loop(8, 11, last_steps, 0)

    l_send = pltpu.make_async_remote_copy(ln.at[half, :], ln.at[half, :], own_s.at[2], own_r.at[2], device_id={'tensor': mate})
    l_send.start()

    last = ICI - 1
    g = 4 + last
    slot = last % 2
    cols = group(jnp.int32(g), True)
    arrive(last)
    for c in rr_loads(cols, slot):
        c.wait()
    x_part(g, slot, False, 0, TW)
    mate_copy(last).wait_recv()

    def x_last(n, _):
        for h in range(2):
            c = pl.ds(pl.multiple_of(n * TW + h * GW, TW), TW)
            part = dot(gg[g, :, lanes(1, TW)], rr[slot, c, lanes(1, TW)], NT)
            gg[2 + h, :, pl.ds(pl.multiple_of(n * TW, TW), TW)] = (dd[:, c] + part).astype(BF16)
        return 0

    lax.fori_loop(0, 2, x_last, 0)
    for c in lr_loads:
        c.wait()

    def d_tile(n, total):
        for h in range(2):
            src = pl.ds(pl.multiple_of(n * TW, TW), TW)
            c = pl.ds(pl.multiple_of(n * TW + h * GW, TW), TW)
            part = dot(gg[0], gg[2 + h, 0:GW, src], NN) + dot(gg[1], gg[2 + h, GW:N, src], NN)
            dd[:, c] = part
            total = total + jnp.sum(part * part, axis=0, keepdims=True)
        return total

    dir_sum = jnp.sum(lax.fori_loop(0, 2, d_tile, jnp.zeros((1, TW), F32)))
    mine[0] = jnp.full((8, CW), adam_sum, F32)
    mine[1] = jnp.full((8, CW), dir_sum, F32)
    r_part(g, 0, cols)

    def norm_copy(k, slot_of, to):
        return pltpu.make_async_remote_copy(mine, sums.at[slot_of], n_s.at[k], n_r.at[k], device_id={'tensor': to})

    for k in range(1, NDEV):
        norm_copy(NDEV - 1 - k, NDEV - 1 - k, lax.rem(me + k, NDEV)).start()
    r_part(g, 1, cols)
    l_send.wait()
    l_part(g, pl.ds(0, GW))
    l_part(g, pl.ds(GW, GW))
    for k in range(1, NDEV):
        norm_copy(k - 1, k - 1, lax.rem(me + k, NDEV)).wait_recv()

    a_all = mine[0]
    d_all = mine[1]
    for k in range(NDEV - 1):
        a_all = a_all + sums[k, 0]
        d_all = d_all + sums[k, 1]
    ratio[...] = jnp.sqrt(a_all / d_all)

    for k in range(1, NDEV):
        norm_copy(NDEV - 1 - k, NDEV - 1 - k, lax.rem(me + k, NDEV)).wait_send()
    for j in range(4):
        x_copy(8 + j, gg.at[4 + j, :, lanes(1)]).wait_send()
        y_copy(8 + j, gg.at[4 + j, :, lanes(0)]).wait_send()
    for i in range(ICI):
        mate_copy(i).wait_send()


def write_kernel(r0, r1, r2, r3, r4, r5, r6, r7, dd, ln, ratio, g_hbm, v_hbm, l_out, r_out, d_out, v_out,
                 vbuf, gbuf, dbuf, in_sem, out_sem):
    loads = [pltpu.make_async_copy(v_hbm, vbuf, in_sem.at[0]), pltpu.make_async_copy(g_hbm, gbuf, in_sem.at[1])]
    for c in loads:
        c.start()
    stores = []

    def store(src, dst):
        c = pltpu.make_async_copy(src, dst, out_sem.at[len(stores)])
        c.start()
        stores.append(c)

    me = lax.axis_index('tensor')
    xpos = lax.rem(lax.div(me, 2), 2)
    mate = me + 1 - 2 * lax.rem(me, 2)
    xhop, yhop = 2 - 4 * xpos, 4 - 8 * lax.div(me, 4)
    blocks = (me, mate, me + xhop, me + yhop, mate + xhop, mate + yhop, me + xhop + yhop, mate + xhop + yhop)
    for src, dev in zip((r0, r1, r2, r3, r4, r5, r6, r7), blocks):
        store(src, r_out.at[:, pl.ds(pl.multiple_of(dev * N, N), N)])
    store(ln, l_out)
    scale = ratio[0:1, 0:1]

    def scaled(k, _):
        rows = pl.ds(pl.multiple_of(k * 64, 64), 64)
        dbuf[rows, :] = dd[rows, :] * scale
        return 0

    lax.fori_loop(0, N // 64, scaled, 0)
    store(dbuf, d_out)
    for c in loads:
        c.wait()

    def moment(k, _):
        rows = pl.ds(pl.multiple_of(k * 64, 64), 64)
        grad = gbuf[rows, :].astype(F32)
        vbuf[rows, :] = EMA_DECAY * vbuf[rows, :] + (1.0 - EMA_DECAY) * grad * grad
        return 0

    lax.fori_loop(0, N // 64, moment, 0)
    store(vbuf, v_out)
    for c in stores:
        c.wait()


def solution(mesh):
    col_spec = P('layer', 'tensor')
    rep_spec = P('layer', None)
    row_spec = P(('layer', 'tensor'), None)
    hbm = pl.BlockSpec(memory_space=pl.ANY)
    vmem = pl.BlockSpec(memory_space=pltpu.VMEM)
    dma = pltpu.SemaphoreType.DMA

    def local_step(grad_loc, left_stat, right_loc, left_root, root_loc, moment_loc):
        mids = pl.pallas_call(
            gather_kernel,
            name='gather_compute',
            out_shape=(pltpu.VMEM((N, N), F32),) * (NDEV + 2) + (pltpu.VMEM((8, CW), F32),),
            in_specs=[hbm] * 6,
            out_specs=(vmem,) * (NDEV + 3),
            scratch_shapes=[
                pltpu.VMEM((16, N, GW), BF16),
                pltpu.VMEM((N, N), BF16),
                pltpu.VMEM((2, N, GW), BF16),
                pltpu.VMEM((2, 8, CW), F32),
                pltpu.VMEM((NDEV - 1, 2, 8, CW), F32),
                dma((4,)), dma((8,)), dma((2, 4)), dma((2,)),
                dma((3,)), dma((3,)), dma((ICI,)), dma((ICI,)), dma((ICI,)), dma((ICI,)),
                dma((ICI,)), dma((ICI,)), dma((NDEV - 1,)), dma((NDEV - 1,)),
            ],
            compiler_params=pltpu.CompilerParams(collective_id=0, has_side_effects=True, vmem_limit_bytes=VM1),
            cost_estimate=pl.CostEstimate(flops=46 * 2**30, bytes_accessed=60 * 2**20, transcendentals=2**20),
        )(grad_loc, left_stat, right_loc, left_root, root_loc, moment_loc)
        left_new, right_new, direction, moment_new = pl.pallas_call(
            write_kernel,
            name='write_results',
            out_shape=(jax.ShapeDtypeStruct((N, N), F32), jax.ShapeDtypeStruct((N, NDEV * N), F32),
                       jax.ShapeDtypeStruct((N, N), F32), jax.ShapeDtypeStruct((N, N), F32)),
            in_specs=[vmem] * (NDEV + 3) + [pl.BlockSpec(memory_space=pltpu.HBM)] * 2,
            out_specs=(hbm,) * 4,
            scratch_shapes=[pltpu.VMEM((N, N), F32), pltpu.VMEM((N, N), BF16), pltpu.VMEM((N, N), F32), dma((2,)), dma((16,))],
            compiler_params=pltpu.CompilerParams(vmem_limit_bytes=VM2),
        )(*(pltpu.with_memory_space_constraint(t, pltpu.VMEM) for t in mids), grad_loc, moment_loc)
        return left_new, right_new, direction, moment_new

    return jax.shard_map(local_step, mesh=mesh, in_specs=(col_spec, rep_spec, row_spec, rep_spec, row_spec, col_spec),
                         out_specs=(rep_spec, row_spec, col_spec, col_spec), check_vma=False)


VM1 = 23 * 2**20
VM2 = VM1
```

time: 257 us -> 130 us (0.51)
  Pallas kernels: 0 us -> 129 us
  waiting for transfers between devices: 120 us -> 0 us
  matrix products: 72 us -> 0 us
  blocking collectives: 22.5 us -> 0 us
  other arithmetic: 21.1 us -> 0 us
  between operations: 15.4 us -> 0.8 us
  local copies, waits for them, and re-layouts: 5.94 us -> 0 us
    pallas_call x0 -> x2, Pallas kernels: none -> 129 us  [the longest x1 112 us: local_step(): pl.pallas_call(gather_kernel, name='gather_compute', out_shape=(pltpu.VME...]
    all_gather x1 -> x0, waiting for transfers between devices: 74.4 us -> none  [local_step(): grad_full = lax.all_gather(grad_loc, 'tensor', axis=1, tiled=True)]
    dot_general x4 -> x0, matrix products: 72 us -> none  [the longest x1 38.2 us: local_step(): lax.dot_general(grad_loc, grad_full, (((0,), (0,)), ((), ())), preferred_...]
    psum x1 -> x0, waiting for transfers between devices: 44.6 us -> none  [local_step(): left_sum = lax.psum(left_part, 'tensor')]
    psum x1 -> x0, blocking collectives: 22.5 us -> none  [local_step(): total_sq = lax.psum(local_sq, 'tensor')]
    reduce_sum x1 -> x0, other arithmetic: 7.76 us -> none  [local_step(): jnp.sum(adam_dir * adam_dir)]
    add x1 -> x0, other arithmetic: 6.97 us -> none  [local_step(): left_new = EMA_DECAY * left_stat + (1.0 - EMA_DECAY) * left_sum]
    unnamed x5 -> x0, local copies, waits for them, and re-layouts: 5.35 us -> none
  transfers between devices with their start and end apart: 2 -> 0, of which waited for: 2 -> 0; matrix products, arithmetic and copies ran while one was open for 17% -> 0% of each run, Pallas kernels for 0% -> 0%
where the time goes in v2:
time: 130 us
  Pallas kernels  129 us (99%)
    pallas_call x1, Pallas kernels, local_step(): pl.pallas_call(gather_kernel, name='gather_compute', out_shape=(pltpu.VME...  112 us
    pallas_call x1, Pallas kernels, local_step(): pl.pallas_call(write_kernel, name='write_results', out_shape=(jax.ShapeDt...  16.5 us

profile of v2, /device:TPU:0, one launch (start us, length us, event | category | flops | bytes accessed | tf_op | source)
XLA Modules:
  0.0 129.7 jit_solution(5711983777538793660)
XLA Ops:
  0.6 112.4 %gather_compute.1 = (f32[1024,1024]{1,0:T(8,128)S(1)}, f32[1024,1024]{1,0:T(8,128)S(1)}, f32[1024,1024]{1,0:T(8,128)S(1)}, f32[1024,1024]{1,0:T(8,128)S(1)}, f32...) custom-call(bf16[1024,1024]{1,0:T(8,128)(2,1)} %g_hbm.3, ...), custom_call_target="tpu_custom_call" | custom-call | flops 49392123904 | bytes 62914560 | tf_op jit(solution)/shard_map/gather_compute/pallas_call | solution.py:359
  113.1 16.5 %write_results.1 = (f32[1024,1024]{1,0:T(8,128)}, f32[1024,8192]{1,0:T(8,128)}, f32[1024,1024]{1,0:T(8,128)}, f32[1024,1024]{1,0:T(8,128)}) custom-call(f32[1024,1024]{1,0:T(8,128)S(1)} %get-tuple-element.15.r0, f32[1024,1024]{1,0:T(8,128)S(1)} %get-tuple-element.16.r1, f32[1024,1024]{1,0:T(8,128)S(1)} %get-tuple-element.17.r2, ...), custom_call_target="tpu_custom_call" | custom-call | tf_op jit(solution)/shard_map/write_results/pallas_call | solution.py:378

commit v3 on v2

v3 whole, which is shorter than its diff:
```python
import jax
import jax.numpy as jnp
from jax import lax
from jax.experimental import pallas as pl
from jax.experimental.pallas import tpu as pltpu
from jax.sharding import PartitionSpec as P

EMA_DECAY = 0.9
ADAM_EPS = 1e-8
N = 1024
CW = 128
GW = 512
TW = 256
NDEV = 8
ICI = 12
EARLY = 4
F32 = jnp.float32
BF16 = jnp.bfloat16

NT = (((1,), (1,)), ((), ()))
NN = (((1,), (0,)), ((), ()))


def dot(a, b, dims):
    return lax.dot_general(a, b, dims, preferred_element_type=F32)


def gather_kernel(g_hbm, l_hbm, r_hbm, lr_hbm, rr_hbm, v_hbm,
                  rn, dd, ln, ratio,
                  gg, gt, rr, mine, sums,
                  load_sem, rload_sem, rr_sem, lr_sem,
                  own_s, own_r, x_s, x_r, y_s, y_r, p_s, p_r, n_s, n_r):
    me = lax.axis_index('tensor')
    core = lax.rem(me, 2)
    xhop = 2 - 4 * lax.rem(lax.div(me, 2), 2)
    yhop = 4 - 8 * lax.div(me, 4)
    mate = me + 1 - 2 * core
    xnb = me + xhop
    ynb = me + yhop

    def device(b):
        q = b // 2
        return me + (b % 2) * (mate - me) + (q % 2) * xhop + (q // 2) * yhop

    def pieces(g):
        i = g - 4
        late = i // 8
        xc, yc = (i + 4 * (1 - late)) % 8, i - 4 * late
        bx, by = 2 + 4 * late, 4 + 2 * late
        return [(bx, xc), (by, yc), (bx + 1, xc), (by + 1, yc)]

    def local_pieces(g):
        return [(g // 2, (g % 2) * 4 + j) for j in range(4)]

    def lanes(j, w=CW):
        return pl.ds(j * w, w)

    own_loads = [pltpu.make_async_copy(g_hbm.at[:, h * GW:(h + 1) * GW], gg.at[h], load_sem.at[h]) for h in range(2)]
    v_load = pltpu.make_async_copy(v_hbm, dd, load_sem.at[2])
    half = pl.ds(pl.multiple_of(core * GW, GW), GW)
    l_load = pltpu.make_async_copy(l_hbm.at[half, :], ln.at[half, :], load_sem.at[3])
    for c in own_loads:
        c.start()

    r_loads = [pltpu.make_async_copy(r_hbm.at[:, pl.ds(pl.multiple_of(device(b) * N, N), N)], rn.at[b], rload_sem.at[b])
               for b in range(NDEV)]

    def rr_loads(where, slot):
        return [pltpu.make_async_copy(rr_hbm.at[:, pl.ds(pl.multiple_of(device(b) * N + c * CW, CW), CW)],
                                      rr.at[slot, :, lanes(j)], rr_sem.at[slot, j]) for j, (b, c) in enumerate(where)]

    barrier = pltpu.get_barrier_semaphore()
    for k in range(1, NDEV):
        pl.semaphore_signal(barrier, inc=1, device_id={'tensor': lax.rem(me + k, NDEV)})
    v_load.start()
    for c in rr_loads(local_pieces(0), 0):
        c.start()
    r_loads[0].start()
    l_load.start()
    r_loads[1].start()
    for c in own_loads:
        c.wait()
    pl.semaphore_wait(barrier, NDEV - 1)

    def own_send(h):
        return pltpu.make_async_remote_copy(gg.at[h], gg.at[2 + h], own_s.at[h], own_r.at[h], device_id={'tensor': mate})

    def x_copy(n, src):
        return pltpu.make_async_remote_copy(src, gg.at[4 + n, :, lanes(0)], x_s.at[n], x_r.at[n], device_id={'tensor': xnb})

    def y_copy(n, src):
        return pltpu.make_async_remote_copy(src, gg.at[4 + n, :, lanes(1)], y_s.at[n], y_r.at[n], device_id={'tensor': ynb})

    def own_chunk(c):
        return gg.at[c // 4, :, pl.ds(pl.multiple_of((c % 4) * CW, CW), CW)]

    def send_own(n):
        x_copy(n, own_chunk((n + 4) % 8)).start()
        y_copy(n, own_chunk(n)).start()

    def send_forward(j):
        x_copy(8 + j, gg.at[4 + j, :, lanes(1)]).start()
        y_copy(8 + j, gg.at[4 + j, :, lanes(0)]).start()

    def mate_copy(i):
        return pltpu.make_async_remote_copy(gg.at[4 + i, :, lanes(0, TW)], gg.at[4 + i, :, lanes(1, TW)],
                                            p_s.at[i], p_r.at[i], device_id={'tensor': mate})

    for n in range(EARLY):
        send_own(n)
    for h in range(2):
        own_send(h).start()
    for c in r_loads[2:]:
        c.start()

    v_load.wait()

    def adam(k, total):
        rows = pl.ds(pl.multiple_of(k * 64, 64), 64)
        for h in range(2):
            grad = gg[h, rows, :].astype(F32)
            moment = EMA_DECAY * dd[rows, lanes(h, GW)] + (1.0 - EMA_DECAY) * grad * grad
            a = grad / (jnp.sqrt(moment) + ADAM_EPS)
            dd[rows, lanes(h, GW)] = jnp.zeros((64, GW), F32)
            total = total + jnp.sum(a * a, axis=0, keepdims=True)
        return total

    adam_sum = jnp.sum(lax.fori_loop(0, N // 64, adam, jnp.zeros((1, GW), F32)))

    def transpose(k, _):
        rows = pl.ds(pl.multiple_of(k * CW, CW), CW)
        for h in range(2):
            gt[lanes(h, GW), rows] = gg[h, rows, :].T
        return 0

    lax.fori_loop(0, N // CW, transpose, 0)

    def x_part(g, slot):
        for n in range(N // TW):
            cols = lanes(n, TW)
            dd[:, cols] = dd[:, cols] + dot(gg[g], rr[slot, cols, :], NT)

    def r_part(g, h, where):
        part = (1.0 - EMA_DECAY) * dot(gt[...], gg[g, :, lanes(h, TW)], NN)
        for j in range(2):
            b, c = where[2 * h + j]
            cols = pl.ds(pl.multiple_of(c * CW, CW), CW)
            rn[b, :, cols] = EMA_DECAY * rn[b, :, cols] + part[:, j * CW:(j + 1) * CW]

    def l_part(g, rows):
        for n in range(N // TW):
            cols = lanes(n, TW)
            ln[rows, cols] = ln[rows, cols] + (1.0 - EMA_DECAY) * dot(gg[g, rows, :], gg[g, cols, :], NT)

    l_load.wait()

    def decay(k, _):
        rows = pl.ds(pl.multiple_of(core * GW + k * 64, 64), 64)
        ln[rows, :] = EMA_DECAY * ln[rows, :]
        return 0

    lax.fori_loop(0, GW // 64, decay, 0)
    r_loads[0].wait()

    def arrive(i):
        x_copy(i, gg.at[4 + i, :, lanes(0)]).wait_recv()
        y_copy(i, gg.at[4 + i, :, lanes(1)]).wait_recv()
        mate_copy(i).start()

    def local_step(g, _):
        slot = g % 2
        where = local_pieces(g)

        @pl.when(g < 3)
        def _():
            for c in rr_loads(local_pieces(g + 1), 1 - slot):
                c.start()

        @pl.when(g == 3)
        def _():
            for c in rr_loads(pieces(g + 1), 1 - slot):
                c.start()

        @pl.when(g >= 2)
        def _():
            own_send(g - 2).wait()

        @pl.when(g == 2)
        def _():
            r_loads[1].wait()

        for c in rr_loads(where, slot):
            c.wait()
        r_part(g, 0, where)
        r_part(g, 1, where)
        x_part(g, slot)
        l_part(g, half)
        return 0

    lax.fori_loop(0, 4, local_step, 0)
    for c in r_loads[2:]:
        c.wait()

    lr_loads = [pltpu.make_async_copy(lr_hbm.at[:, h * GW:(h + 1) * GW], gg.at[h], lr_sem.at[h]) for h in range(2)]

    def step(i, _):
        g = 4 + i
        slot = i % 2
        where = pieces(g)
        for c in rr_loads(pieces(g + 1), 1 - slot):
            c.start()
        arrive(i)

        @pl.when(i < 8 - EARLY)
        def _():
            send_own(i + EARLY)

        @pl.when((i >= 8 - EARLY) & (i < ICI - EARLY))
        def _():
            send_forward(i + EARLY - 8)

        @pl.when(i == 9)
        def _():
            for n in range(8):
                x_copy(n, own_chunk((n + 4) % 8)).wait_send()
                y_copy(n, own_chunk(n)).wait_send()
            for c in lr_loads:
                c.start()

        r_part(g, 0, where)
        mate_copy(i).wait_recv()
        for c in rr_loads(where, slot):
            c.wait()
        r_part(g, 1, where)
        x_part(g, slot)
        l_part(g, half)
        return 0

    last = ICI - 1
    lax.fori_loop(0, last, step, 0)

    l_send = pltpu.make_async_remote_copy(ln.at[half, :], ln.at[half, :], own_s.at[2], own_r.at[2], device_id={'tensor': mate})
    l_send.start()

    g = 4 + last
    slot = last % 2
    where = pieces(g)
    arrive(last)
    for c in rr_loads(where, slot):
        c.wait()
    for n in range(N // TW):
        cols = lanes(n, TW)
        dd[:, cols] = dd[:, cols] + dot(gg[g, :, lanes(0, TW)], rr[slot, cols, lanes(0, TW)], NT)
    mate_copy(last).wait_recv()
    for n in range(N // TW):
        cols = lanes(n, TW)
        part = dot(gg[g, :, lanes(1, TW)], rr[slot, cols, lanes(1, TW)], NT)
        gg[2 + n // 2, :, lanes(n % 2, TW)] = (dd[:, cols] + part).astype(BF16)
    for c in lr_loads:
        c.wait()
    total = jnp.zeros((1, TW), F32)
    for n in range(N // TW):
        src = lanes(n % 2, TW)
        part = dot(gg[0], gg[2 + n // 2, 0:GW, src], NN) + dot(gg[1], gg[2 + n // 2, GW:N, src], NN)
        dd[:, lanes(n, TW)] = part
        total = total + jnp.sum(part * part, axis=0, keepdims=True)
    mine[0] = jnp.full((8, CW), adam_sum, F32)
    mine[1] = jnp.full((8, CW), jnp.sum(total), F32)
    r_part(g, 0, where)

    def norm_copy(k, slot_of, to):
        return pltpu.make_async_remote_copy(mine, sums.at[slot_of], n_s.at[k], n_r.at[k], device_id={'tensor': to})

    for k in range(1, NDEV):
        norm_copy(NDEV - 1 - k, NDEV - 1 - k, lax.rem(me + k, NDEV)).start()
    r_part(g, 1, where)
    l_send.wait()
    l_part(g, pl.ds(0, N))
    for k in range(1, NDEV):
        norm_copy(k - 1, k - 1, lax.rem(me + k, NDEV)).wait_recv()

    a_all = mine[0]
    d_all = mine[1]
    for k in range(NDEV - 1):
        a_all = a_all + sums[k, 0]
        d_all = d_all + sums[k, 1]
    ratio[...] = jnp.sqrt(a_all / d_all)

    for k in range(1, NDEV):
        norm_copy(NDEV - 1 - k, NDEV - 1 - k, lax.rem(me + k, NDEV)).wait_send()
    for j in range(4):
        x_copy(8 + j, gg.at[4 + j, :, lanes(1)]).wait_send()
        y_copy(8 + j, gg.at[4 + j, :, lanes(0)]).wait_send()
    for i in range(ICI):
        mate_copy(i).wait_send()


def write_kernel(rn, dd, ln, ratio, g_hbm, v_hbm, l_out, r_out, d_out, v_out,
                 vbuf, gbuf, dbuf, in_sem, out_sem):
    loads = [pltpu.make_async_copy(v_hbm, vbuf, in_sem.at[0]), pltpu.make_async_copy(g_hbm, gbuf, in_sem.at[1])]
    for c in loads:
        c.start()
    stores = []

    def store(src, dst):
        c = pltpu.make_async_copy(src, dst, out_sem.at[len(stores)])
        c.start()
        stores.append(c)

    me = lax.axis_index('tensor')
    to_mate = 1 - 2 * lax.rem(me, 2)
    xhop, yhop = 2 - 4 * lax.rem(lax.div(me, 2), 2), 4 - 8 * lax.div(me, 4)
    for b in range(NDEV):
        dev = me + (b % 2) * to_mate + (b // 2 % 2) * xhop + (b // 4) * yhop
        store(rn.at[b], r_out.at[:, pl.ds(pl.multiple_of(dev * N, N), N)])
    store(ln, l_out)
    scale = ratio[0:1, 0:1]

    def scaled(k, _):
        rows = pl.ds(pl.multiple_of(k * 64, 64), 64)
        dbuf[rows, :] = dd[rows, :] * scale
        return 0

    lax.fori_loop(0, N // 64, scaled, 0)
    store(dbuf, d_out)
    for c in loads:
        c.wait()

    def moment(k, _):
        rows = pl.ds(pl.multiple_of(k * 64, 64), 64)
        grad = gbuf[rows, :].astype(F32)
        vbuf[rows, :] = EMA_DECAY * vbuf[rows, :] + (1.0 - EMA_DECAY) * grad * grad
        return 0

    lax.fori_loop(0, N // 64, moment, 0)
    store(vbuf, v_out)
    for c in stores:
        c.wait()


def solution(mesh):
    col_spec = P('layer', 'tensor')
    rep_spec = P('layer', None)
    row_spec = P(('layer', 'tensor'), None)
    hbm = pl.BlockSpec(memory_space=pl.ANY)
    vmem = pl.BlockSpec(memory_space=pltpu.VMEM)
    dma = pltpu.SemaphoreType.DMA

    def local_step(grad_loc, left_stat, right_loc, left_root, root_loc, moment_loc):
        mids = pl.pallas_call(
            gather_kernel,
            name='gather_compute',
            out_shape=(pltpu.VMEM((NDEV, N, N), F32), pltpu.VMEM((N, N), F32), pltpu.VMEM((N, N), F32), pltpu.VMEM((8, CW), F32)),
            in_specs=[hbm] * 6,
            out_specs=(vmem,) * 4,
            scratch_shapes=[
                pltpu.VMEM((16, N, GW), BF16),
                pltpu.VMEM((N, N), BF16),
                pltpu.VMEM((2, N, GW), BF16),
                pltpu.VMEM((2, 8, CW), F32),
                pltpu.VMEM((NDEV - 1, 2, 8, CW), F32),
                dma((4,)), dma((8,)), dma((2, 4)), dma((2,)),
                dma((3,)), dma((3,)), dma((ICI,)), dma((ICI,)), dma((ICI,)), dma((ICI,)),
                dma((ICI,)), dma((ICI,)), dma((NDEV - 1,)), dma((NDEV - 1,)),
            ],
            compiler_params=pltpu.CompilerParams(collective_id=0, has_side_effects=True, vmem_limit_bytes=VM1),
            cost_estimate=pl.CostEstimate(flops=46 * 2**30, bytes_accessed=60 * 2**20, transcendentals=2**20),
        )(grad_loc, left_stat, right_loc, left_root, root_loc, moment_loc)
        left_new, right_new, direction, moment_new = pl.pallas_call(
            write_kernel,
            name='write_results',
            out_shape=(jax.ShapeDtypeStruct((N, N), F32), jax.ShapeDtypeStruct((N, NDEV * N), F32),
                       jax.ShapeDtypeStruct((N, N), F32), jax.ShapeDtypeStruct((N, N), F32)),
            in_specs=[vmem] * 4 + [pl.BlockSpec(memory_space=pltpu.HBM)] * 2,
            out_specs=(hbm,) * 4,
            scratch_shapes=[pltpu.VMEM((N, N), F32), pltpu.VMEM((N, N), BF16), pltpu.VMEM((N, N), F32), dma((2,)), dma((16,))],
            compiler_params=pltpu.CompilerParams(vmem_limit_bytes=VM2),
        )(*(pltpu.with_memory_space_constraint(t, pltpu.VMEM) for t in mids), grad_loc, moment_loc)
        return left_new, right_new, direction, moment_new

    return jax.shard_map(local_step, mesh=mesh, in_specs=(col_spec, rep_spec, row_spec, rep_spec, row_spec, col_spec),
                         out_specs=(rep_spec, row_spec, col_spec, col_spec), check_vma=False)


VM1 = 23 * 2**20
VM2 = VM1
```

time: 130 us -> 109 us (0.84)
  Pallas kernels: 129 us -> 108 us
    pallas_call x1, Pallas kernels: 112 us -> 92 us  [local_step(): pl.pallas_call(gather_kernel, name='gather_compute', out_shape=(pltpu.VME...]
where the time goes in v3:
time: 109 us
  Pallas kernels  108 us (99%)
    pallas_call x1, Pallas kernels, local_step(): pl.pallas_call(gather_kernel, name='gather_compute', out_shape=(pltpu.VME...  92 us
    pallas_call x1, Pallas kernels, local_step(): pl.pallas_call(write_kernel, name='write_results', out_shape=(jax.ShapeDt...  16.5 us

profile of v3, /device:TPU:0, one launch (start us, length us, event | category | flops | bytes accessed | tf_op | source)
XLA Modules:
  0.0 109.1 jit_solution(4075602536884716231)
XLA Ops:
  0.6 92.0 %gather_compute.1 = (f32[8,1024,1024]{2,1,0:T(8,128)S(1)}, f32[1024,1024]{1,0:T(8,128)S(1)}, f32[1024,1024]{1,0:T(8,128)S(1)}, f32[8,128]{1,0:T(8,128)S(1)}) custom-call(bf16[1024,1024]{1,0:T(8,128)(2,1)} %g_hbm.3, f32[1024,1024]{1,0:T(8,128)} %l_hbm.1, f32[1024,8192]{1,0:T(8,128)} %r_hbm.1, bf16[1024,1024]{1,0:T(8,128)(2,1)} %lr_hbm.1, ...), custom_call_target="tpu_custom_call" | custom-call | flops 49392123904 | bytes 62914560 | tf_op jit(solution)/shard_map/gather_compute/pallas_call | solution.py:350
  92.6 16.5 %write_results.1 = (f32[1024,1024]{1,0:T(8,128)}, f32[1024,8192]{1,0:T(8,128)}, f32[1024,1024]{1,0:T(8,128)}, f32[1024,1024]{1,0:T(8,128)}) custom-call(f32[8,1024,1024]{2,1,0:T(8,128)S(1)} %get-tuple-element.8.rn, f32[1024,1024]{1,0:T(8,128)S(1)} %get-tuple-element.9.dd, f32[1024,1024]{1,0:T(8,128)S(1)} %get-tuple-element.10.ln, ...), custom_call_target="tpu_custom_call" | custom-call | tf_op jit(solution)/shard_map/write_results/pallas_call | solution.py:369

commit v4 on v3

v4 whole, which is shorter than its diff:
```python
import jax
import jax.numpy as jnp
from jax import lax
from jax.experimental import pallas as pl
from jax.experimental.pallas import tpu as pltpu
from jax.sharding import PartitionSpec as P

EMA_DECAY = 0.9
ADAM_EPS = 1e-8
N = 1024
CW = 128
GW = 512
TW = 256
NDEV = 8
ICI = 12
EARLY = 4
RING = 4
F32 = jnp.float32
BF16 = jnp.bfloat16

NT = (((1,), (1,)), ((), ()))
NN = (((1,), (0,)), ((), ()))


def dot(a, b, dims):
    return lax.dot_general(a, b, dims, preferred_element_type=F32)


def gather_kernel(g_hbm, l_hbm, r_hbm, lr_hbm, rr_hbm, v_hbm,
                  rn, dd, ln, vn, ratio,
                  gl, gi, gm, gt, rr, mine, sums,
                  load_sem, rload_sem, rr_sem, lr_sem,
                  own_s, own_r, x_s, x_r, y_s, y_r, p_s, p_r, n_s, n_r, credit):
    me = lax.axis_index('tensor')
    core = lax.rem(me, 2)
    xhop = 2 - 4 * lax.rem(lax.div(me, 2), 2)
    yhop = 4 - 8 * lax.div(me, 4)
    mate = me + 1 - 2 * core
    xnb = me + xhop
    ynb = me + yhop

    def device(b):
        q = b // 2
        return me + (b % 2) * (mate - me) + (q % 2) * xhop + (q // 2) * yhop

    def pieces(g):
        i = g - 4
        late = i // 8
        xc, yc = (i + 4 * (1 - late)) % 8, i - 4 * late
        bx, by = 2 + 4 * late, 4 + 2 * late
        return [(bx, xc), (by, yc), (bx + 1, xc), (by + 1, yc)]

    def local_pieces(g):
        return [(g // 2, (g % 2) * 4 + j) for j in range(4)]

    def lanes(j, w=CW):
        return pl.ds(j * w, w)

    own_loads = [pltpu.make_async_copy(g_hbm.at[:, h * GW:(h + 1) * GW], gl.at[h], load_sem.at[h]) for h in range(2)]
    v_load = pltpu.make_async_copy(v_hbm, vn, load_sem.at[2])
    half = pl.ds(pl.multiple_of(core * GW, GW), GW)
    l_load = pltpu.make_async_copy(l_hbm.at[half, :], ln.at[half, :], load_sem.at[3])
    for c in own_loads:
        c.start()

    r_loads = [pltpu.make_async_copy(r_hbm.at[:, pl.ds(pl.multiple_of(device(b) * N, N), N)], rn.at[b], rload_sem.at[b])
               for b in range(NDEV)]

    def rr_loads(where, slot):
        return [pltpu.make_async_copy(rr_hbm.at[:, pl.ds(pl.multiple_of(device(b) * N + c * CW, CW), CW)],
                                      rr.at[slot, :, lanes(j)], rr_sem.at[slot, j]) for j, (b, c) in enumerate(where)]

    barrier = pltpu.get_barrier_semaphore()
    for k in range(1, NDEV):
        pl.semaphore_signal(barrier, inc=1, device_id={'tensor': lax.rem(me + k, NDEV)})
    v_load.start()
    for c in rr_loads(local_pieces(0), 0):
        c.start()
    r_loads[0].start()
    l_load.start()
    r_loads[1].start()
    for c in own_loads:
        c.wait()
    pl.semaphore_wait(barrier, NDEV - 1)

    def own_send(h):
        return pltpu.make_async_remote_copy(gl.at[h], gl.at[2 + h], own_s.at[h], own_r.at[h], device_id={'tensor': mate})

    def x_copy(n, src):
        return pltpu.make_async_remote_copy(src, gi.at[n, :, lanes(0)], x_s.at[n], x_r.at[n], device_id={'tensor': xnb})

    def y_copy(n, src):
        return pltpu.make_async_remote_copy(src, gi.at[n, :, lanes(1)], y_s.at[n], y_r.at[n], device_id={'tensor': ynb})

    def own_chunk(c):
        return gl.at[c // 4, :, pl.ds(pl.multiple_of((c % 4) * CW, CW), CW)]

    def send_own(n):
        x_copy(n, own_chunk((n + 4) % 8)).start()
        y_copy(n, own_chunk(n)).start()

    def send_forward(j):
        x_copy(8 + j, gi.at[j, :, lanes(1)]).start()
        y_copy(8 + j, gi.at[j, :, lanes(0)]).start()

    def mate_copy(i):
        return pltpu.make_async_remote_copy(gi.at[i], gm.at[i % RING], p_s.at[i], p_r.at[i], device_id={'tensor': mate})

    for n in range(EARLY):
        send_own(n)
    for h in range(2):
        own_send(h).start()
    for c in r_loads[2:]:
        c.start()

    v_load.wait()

    def adam(k, total):
        rows = pl.ds(pl.multiple_of(k * 64, 64), 64)
        for h in range(2):
            grad = gl[h, rows, :].astype(F32)
            moment = EMA_DECAY * vn[rows, lanes(h, GW)] + (1.0 - EMA_DECAY) * grad * grad
            a = grad / (jnp.sqrt(moment) + ADAM_EPS)
            vn[rows, lanes(h, GW)] = moment
            dd[rows, lanes(h, GW)] = jnp.zeros((64, GW), F32)
            total = total + jnp.sum(a * a, axis=0, keepdims=True)
        return total

    adam_sum = jnp.sum(lax.fori_loop(0, N // 64, adam, jnp.zeros((1, GW), F32)))

    def transpose(k, _):
        rows = pl.ds(pl.multiple_of(k * CW, CW), CW)
        for h in range(2):
            gt[lanes(h, GW), rows] = gl[h, rows, :].T
        return 0

    lax.fori_loop(0, N // CW, transpose, 0)

    def x_part(halves, slot):
        for n in range(N // TW):
            cols = lanes(n, TW)
            part = sum(dot(a[...], rr[slot, cols, lanes(h, TW)], NT) for h, a in enumerate(halves))
            dd[:, cols] = dd[:, cols] + part

    def r_part(a, where):
        part = (1.0 - EMA_DECAY) * dot(gt[...], a[...], NN)
        for j, (b, c) in enumerate(where):
            cols = pl.ds(pl.multiple_of(c * CW, CW), CW)
            rn[b, :, cols] = EMA_DECAY * rn[b, :, cols] + part[:, j * CW:(j + 1) * CW]

    def l_part(halves, rows):
        for n in range(N // TW):
            cols = lanes(n, TW)
            part = sum(dot(a[rows, :], a[cols, :], NT) for a in halves)
            ln[rows, cols] = ln[rows, cols] + (1.0 - EMA_DECAY) * part

    l_load.wait()

    def decay(k, _):
        rows = pl.ds(pl.multiple_of(core * GW + k * 64, 64), 64)
        ln[rows, :] = EMA_DECAY * ln[rows, :]
        return 0

    lax.fori_loop(0, GW // 64, decay, 0)
    r_loads[0].wait()

    def arrive(i):
        x_copy(i, gi.at[i, :, lanes(0)]).wait_recv()
        y_copy(i, gi.at[i, :, lanes(1)]).wait_recv()
        if isinstance(i, int) and i < RING:
            mate_copy(i).start()
            return

        @pl.when(i >= RING)
        def _():
            pl.semaphore_wait(credit, 1)

        mate_copy(i).start()

    def issue(i):
        @pl.when(i < 8 - EARLY)
        def _():
            send_own(i + EARLY)

        @pl.when((i >= 8 - EARLY) & (i < ICI - EARLY))
        def _():
            send_forward(i + EARLY - 8)

    def local_step(g, _):
        slot = g % 2
        where = local_pieces(g)
        halves = [gl.at[g, :, lanes(h, TW)] for h in range(2)]

        @pl.when(g < 3)
        def _():
            for c in rr_loads(local_pieces(g + 1), 1 - slot):
                c.start()

        @pl.when(g == 3)
        def _():
            for c in rr_loads(pieces(4), 0):
                c.start()

        @pl.when(g >= 2)
        def _():
            own_send(g - 2).wait()

        @pl.when(g == 2)
        def _():
            r_loads[1].wait()

        for c in rr_loads(where, slot):
            c.wait()
        x_part(halves, slot)
        r_part(halves[0], where[:2])

        @pl.when(g == 3)
        def _():
            arrive(0)
            issue(0)
            for c in r_loads[2:]:
                c.wait()

        r_part(halves[1], where[2:])
        l_part(halves, half)
        return 0

    lax.fori_loop(0, 4, local_step, 0)

    lr_loads = [pltpu.make_async_copy(lr_hbm.at[:, h * GW:(h + 1) * GW], gl.at[h], lr_sem.at[h]) for h in range(2)]

    def step(i, _):
        slot = i % 2
        where = pieces(4 + i)
        halves = [gi.at[i], gm.at[i % RING]]
        for c in rr_loads(pieces(5 + i), 1 - slot):
            c.start()

        @pl.when(i == 9)
        def _():
            for n in range(8):
                x_copy(n, own_chunk((n + 4) % 8)).wait_send()
                y_copy(n, own_chunk(n)).wait_send()
            for c in lr_loads:
                c.start()

        mate_copy(i).wait_recv()
        for c in rr_loads(where, slot):
            c.wait()
        x_part(halves, slot)
        r_part(halves[0], where[:2])
        arrive(i + 1)
        issue(i + 1)
        r_part(halves[1], where[2:])
        l_part(halves, half)

        @pl.when(i < ICI - RING)
        def _():
            pl.semaphore_signal(credit, inc=1, device_id={'tensor': mate})

        return 0

    last = ICI - 1
    lax.fori_loop(0, last, step, 0)

    l_send = pltpu.make_async_remote_copy(ln.at[half, :], ln.at[half, :], own_s.at[2], own_r.at[2], device_id={'tensor': mate})
    l_send.start()

    slot = last % 2
    where = pieces(4 + last)
    halves = [gi.at[last], gm.at[last % RING]]
    for c in rr_loads(where, slot):
        c.wait()
    mate_copy(last).wait_recv()
    for n in range(N // TW):
        cols = lanes(n, TW)
        part = sum(dot(a[...], rr[slot, cols, lanes(h, TW)], NT) for h, a in enumerate(halves))
        gl[2 + n // 2, :, lanes(n % 2, TW)] = (dd[:, cols] + part).astype(BF16)
    for c in lr_loads:
        c.wait()
    total = jnp.zeros((1, TW), F32)
    for n in range(N // TW):
        src = lanes(n % 2, TW)
        part = dot(gl[0], gl[2 + n // 2, 0:GW, src], NN) + dot(gl[1], gl[2 + n // 2, GW:N, src], NN)
        dd[:, lanes(n, TW)] = part
        total = total + jnp.sum(part * part, axis=0, keepdims=True)
    mine[0] = jnp.full((8, CW), adam_sum, F32)
    mine[1] = jnp.full((8, CW), jnp.sum(total), F32)
    r_part(halves[0], where[:2])

    def norm_copy(k, slot_of, to):
        return pltpu.make_async_remote_copy(mine, sums.at[slot_of], n_s.at[k], n_r.at[k], device_id={'tensor': to})

    for k in range(1, NDEV):
        norm_copy(NDEV - 1 - k, NDEV - 1 - k, lax.rem(me + k, NDEV)).start()
    r_part(halves[1], where[2:])
    l_send.wait()
    l_part(halves, pl.ds(0, N))
    for k in range(1, NDEV):
        norm_copy(k - 1, k - 1, lax.rem(me + k, NDEV)).wait_recv()

    a_all = mine[0]
    d_all = mine[1]
    for k in range(NDEV - 1):
        a_all = a_all + sums[k, 0]
        d_all = d_all + sums[k, 1]
    ratio[...] = jnp.sqrt(a_all / d_all)

    for k in range(1, NDEV):
        norm_copy(NDEV - 1 - k, NDEV - 1 - k, lax.rem(me + k, NDEV)).wait_send()
    for j in range(4):
        x_copy(8 + j, gi.at[j, :, lanes(1)]).wait_send()
        y_copy(8 + j, gi.at[j, :, lanes(0)]).wait_send()
    for i in range(ICI):
        mate_copy(i).wait_send()


def write_kernel(rn, dd, ln, vn, ratio, l_out, r_out, d_out, v_out, dbuf, out_sem):
    stores = []

    def store(src, dst):
        c = pltpu.make_async_copy(src, dst, out_sem.at[len(stores)])
        c.start()
        stores.append(c)

    me = lax.axis_index('tensor')
    to_mate = 1 - 2 * lax.rem(me, 2)
    xhop, yhop = 2 - 4 * lax.rem(lax.div(me, 2), 2), 4 - 8 * lax.div(me, 4)
    for b in range(NDEV):
        dev = me + (b % 2) * to_mate + (b // 2 % 2) * xhop + (b // 4) * yhop
        store(rn.at[b], r_out.at[:, pl.ds(pl.multiple_of(dev * N, N), N)])
    store(ln, l_out)
    store(vn, v_out)
    scale = ratio[0:1, 0:1]

    def scaled(k, _):
        rows = pl.ds(pl.multiple_of(k * 64, 64), 64)
        dbuf[rows, :] = dd[rows, :] * scale
        return 0

    lax.fori_loop(0, N // 64, scaled, 0)
    store(dbuf, d_out)
    for c in stores:
        c.wait()


def solution(mesh):
    col_spec = P('layer', 'tensor')
    rep_spec = P('layer', None)
    row_spec = P(('layer', 'tensor'), None)
    hbm = pl.BlockSpec(memory_space=pl.ANY)
    vmem = pl.BlockSpec(memory_space=pltpu.VMEM)
    dma = pltpu.SemaphoreType.DMA

    def local_step(grad_loc, left_stat, right_loc, left_root, root_loc, moment_loc):
        mids = pl.pallas_call(
            gather_kernel,
            name='gather_compute',
            out_shape=(pltpu.VMEM((NDEV, N, N), F32), pltpu.VMEM((N, N), F32), pltpu.VMEM((N, N), F32), pltpu.VMEM((N, N), F32), pltpu.VMEM((8, CW), F32)),
            in_specs=[hbm] * 6,
            out_specs=(vmem,) * 5,
            scratch_shapes=[
                pltpu.VMEM((4, N, GW), BF16),
                pltpu.VMEM((ICI, N, TW), BF16),
                pltpu.VMEM((RING, N, TW), BF16),
                pltpu.VMEM((N, N), BF16),
                pltpu.VMEM((2, N, GW), BF16),
                pltpu.VMEM((2, 8, CW), F32),
                pltpu.VMEM((NDEV - 1, 2, 8, CW), F32),
                dma((4,)), dma((8,)), dma((2, 4)), dma((2,)),
                dma((3,)), dma((3,)), dma((ICI,)), dma((ICI,)), dma((ICI,)), dma((ICI,)),
                dma((ICI,)), dma((ICI,)), dma((NDEV - 1,)), dma((NDEV - 1,)), pltpu.SemaphoreType.REGULAR,
            ],
            compiler_params=pltpu.CompilerParams(collective_id=0, has_side_effects=True, vmem_limit_bytes=VM1),
            cost_estimate=pl.CostEstimate(flops=46 * 2**30, bytes_accessed=60 * 2**20, transcendentals=2**20),
        )(grad_loc, left_stat, right_loc, left_root, root_loc, moment_loc)
        left_new, right_new, direction, moment_new = pl.pallas_call(
            write_kernel,
            name='write_results',
            out_shape=(jax.ShapeDtypeStruct((N, N), F32), jax.ShapeDtypeStruct((N, NDEV * N), F32),
                       jax.ShapeDtypeStruct((N, N), F32), jax.ShapeDtypeStruct((N, N), F32)),
            in_specs=[vmem] * 5,
            out_specs=(hbm,) * 4,
            scratch_shapes=[pltpu.VMEM((N, N), F32), dma((16,))],
            compiler_params=pltpu.CompilerParams(vmem_limit_bytes=VM2),
        )(*(pltpu.with_memory_space_constraint(t, pltpu.VMEM) for t in mids))
        return left_new, right_new, direction, moment_new

    return jax.shard_map(local_step, mesh=mesh, in_specs=(col_spec, rep_spec, row_spec, rep_spec, row_spec, col_spec),
                         out_specs=(rep_spec, row_spec, col_spec, col_spec), check_vma=False)


VM1 = 19 * 2**20
VM2 = VM1
```

time: 109 us -> 105 us (0.963)
  Pallas kernels: 108 us -> 104 us
    pallas_call x1, Pallas kernels: 92 us -> 89.2 us  [local_step(): pl.pallas_call(gather_kernel, name='gather_compute', out_shape=(pltpu.VME...]
    pallas_call x1, Pallas kernels: 16.5 us -> 14.9 us  [local_step(): pl.pallas_call(write_kernel, name='write_results', out_shape=(jax.ShapeDt...]
where the time goes in v4:
time: 105 us
  Pallas kernels  104 us (99%)
    pallas_call x1, Pallas kernels, local_step(): pl.pallas_call(gather_kernel, name='gather_compute', out_shape=(pltpu.VME...  89.2 us
    pallas_call x1, Pallas kernels, local_step(): pl.pallas_call(write_kernel, name='write_results', out_shape=(jax.ShapeDt...  14.9 us

profile of v4, /device:TPU:0, one launch (start us, length us, event | category | flops | bytes accessed | tf_op | source)
XLA Modules:
  0.0 104.7 jit_solution(5730757729801934253)
XLA Ops:
  0.6 89.2 %gather_compute.1 = (f32[8,1024,1024]{2,1,0:T(8,128)S(1)}, f32[1024,1024]{1,0:T(8,128)S(1)}, f32[1024,1024]{1,0:T(8,128)S(1)}, f32[1024,1024]{1,0:T(8,128)S(1)}, f32[8,128]{1,0:T(8,128)S(1)}) custom-call(bf16[1024,1024]{1,0:T(8,128)(2,1)} %g_hbm.1, f32[1024,1024]{1,0:T(8,128)} %l_hbm.1, f32[1024,8192]{1,0:T(8,128)} %r_hbm.1, bf16[1024,1024]{1,0:T(8,128)(2,1)} %lr_hbm.1, ...), custom_call_target="tpu_custom_call" | custom-call | flops 49392123904 | bytes 62914560 | tf_op jit(solution)/shard_map/gather_compute/pallas_call | solution.py:356
  89.8 14.9 %write_results.1 = (f32[1024,1024]{1,0:T(8,128)}, f32[1024,8192]{1,0:T(8,128)}, f32[1024,1024]{1,0:T(8,128)}, f32[1024,1024]{1,0:T(8,128)}) custom-call(f32[8,1024,1024]{2,1,0:T(8,128)S(1)} %get-tuple-element.9.rn, f32[1024,1024]{1,0:T(8,128)S(1)} %get-tuple-element.10.dd, f32[1024,1024]{1,0:T(8,128)S(1)} %get-tuple-element.11.ln, ...), custom_call_target="tpu_custom_call" | custom-call | tf_op jit(solution)/shard_map/write_results/pallas_call | solution.py:377

commit v5 on v4

--- a/solution.py
+++ b/solution.py
@@ -27,8 +27,8 @@
 
 
 def gather_kernel(g_hbm, l_hbm, r_hbm, lr_hbm, rr_hbm, v_hbm,
-                  rn, dd, ln, vn, ratio,
-                  gl, gi, gm, gt, rr, mine, sums,
+                  rn, dd, ln, vn, ratio, gi, gm, gt,
+                  gl, rr, mine, sums,
                   load_sem, rload_sem, rr_sem, lr_sem,
                   own_s, own_r, x_s, x_r, y_s, y_r, p_s, p_r, n_s, n_r, credit):
     me = lax.axis_index('tensor')
@@ -236,14 +236,6 @@
         for c in rr_loads(pieces(5 + i), 1 - slot):
             c.start()
 
-        @pl.when(i == 9)
-        def _():
-            for n in range(8):
-                x_copy(n, own_chunk((n + 4) % 8)).wait_send()
-                y_copy(n, own_chunk(n)).wait_send()
-            for c in lr_loads:
-                c.start()
-
         mate_copy(i).wait_recv()
         for c in rr_loads(where, slot):
             c.wait()
@@ -253,31 +245,48 @@
         issue(i + 1)
         r_part(halves[1], where[2:])
         l_part(halves, half)
-
-        @pl.when(i < ICI - RING)
-        def _():
-            pl.semaphore_signal(credit, inc=1, device_id={'tensor': mate})
-
+        pl.semaphore_signal(credit, inc=1, device_id={'tensor': mate})
         return 0
 
+    lax.fori_loop(0, 8, step, 0)
+
+    def late_step(i, _):
+        slot = i % 2
+        for c in rr_loads(pieces(5 + i), 1 - slot):
+            c.start()
+
+        @pl.when(i == 9)
+        def _():
+            for n in range(8):
+                x_copy(n, own_chunk((n + 4) % 8)).wait_send()
+                y_copy(n, own_chunk(n)).wait_send()
+            for c in lr_loads:
+                c.start()
+
+        mate_copy(i).wait_recv()
+        for c in rr_loads(pieces(4 + i), slot):
+            c.wait()
+        x_part([gi.at[i], gm.at[i % RING]], slot)
+        arrive(i + 1)
+        l_part([gi.at[i], gm.at[i % RING]], half)
+        return 0
+
     last = ICI - 1
-    lax.fori_loop(0, last, step, 0)
+    lax.fori_loop(8, last, late_step, 0)
 
     l_send = pltpu.make_async_remote_copy(ln.at[half, :], ln.at[half, :], own_s.at[2], own_r.at[2], device_id={'tensor': mate})
     l_send.start()
-
     slot = last % 2
-    where = pieces(4 + last)
-    halves = [gi.at[last], gm.at[last % RING]]
-    for c in rr_loads(where, slot):
+    for c in rr_loads(pieces(4 + last), slot):
+        c.wait()
+    x_part([gi.at[last]], slot)
+    for c in lr_loads:
         c.wait()
     mate_copy(last).wait_recv()
     for n in range(N // TW):
         cols = lanes(n, TW)
-        part = sum(dot(a[...], rr[slot, cols, lanes(h, TW)], NT) for h, a in enumerate(halves))
+        part = dot(gm[last % RING], rr[slot, cols, lanes(1, TW)], NT)
         gl[2 + n // 2, :, lanes(n % 2, TW)] = (dd[:, cols] + part).astype(BF16)
-    for c in lr_loads:
-        c.wait()
     total = jnp.zeros((1, TW), F32)
     for n in range(N // TW):
         src = lanes(n % 2, TW)
@@ -286,16 +295,13 @@
         total = total + jnp.sum(part * part, axis=0, keepdims=True)
     mine[0] = jnp.full((8, CW), adam_sum, F32)
     mine[1] = jnp.full((8, CW), jnp.sum(total), F32)
-    r_part(halves[0], where[:2])
 
     def norm_copy(k, slot_of, to):
         return pltpu.make_async_remote_copy(mine, sums.at[slot_of], n_s.at[k], n_r.at[k], device_id={'tensor': to})
 
     for k in range(1, NDEV):
         norm_copy(NDEV - 1 - k, NDEV - 1 - k, lax.rem(me + k, NDEV)).start()
-    r_part(halves[1], where[2:])
     l_send.wait()
-    l_part(halves, pl.ds(0, N))
     for k in range(1, NDEV):
         norm_copy(k - 1, k - 1, lax.rem(me + k, NDEV)).wait_recv()
 
@@ -315,31 +321,42 @@
         mate_copy(i).wait_send()
 
 
-def write_kernel(rn, dd, ln, vn, ratio, l_out, r_out, d_out, v_out, dbuf, out_sem):
-    stores = []
-
-    def store(src, dst):
-        c = pltpu.make_async_copy(src, dst, out_sem.at[len(stores)])
-        c.start()
-        stores.append(c)
-
+def write_kernel(rn_in, dd_in, ln_in, vn, ratio, gi, gm, gt, l_out, r_out, d_out, v_out, rn, dd, ln, sem):
     me = lax.axis_index('tensor')
     to_mate = 1 - 2 * lax.rem(me, 2)
     xhop, yhop = 2 - 4 * lax.rem(lax.div(me, 2), 2), 4 - 8 * lax.div(me, 4)
-    for b in range(NDEV):
+    stores = []
+
+    def store(src, dst):
+        c = pltpu.make_async_copy(src, dst, sem.at[len(stores)])
+        c.start()
+        stores.append(c)
+
+    def columns(b, c, w):
         dev = me + (b % 2) * to_mate + (b // 2 % 2) * xhop + (b // 4) * yhop
-        store(rn.at[b], r_out.at[:, pl.ds(pl.multiple_of(dev * N, N), N)])
-    store(ln, l_out)
+        return pl.ds(pl.multiple_of(dev * N + c * CW, CW), w)
+
+    for b in range(6):
+        store(rn.at[b], r_out.at[:, columns(b, 0, N)])
     store(vn, v_out)
     scale = ratio[0:1, 0:1]
-
-    def scaled(k, _):
-        rows = pl.ds(pl.multiple_of(k * 64, 64), 64)
-        dbuf[rows, :] = dd[rows, :] * scale
-        return 0
-
-    lax.fori_loop(0, N // 64, scaled, 0)
-    store(dbuf, d_out)
+    for n in range(N // TW):
+        cols = pl.ds(n * TW, TW)
+        dd[:, cols] = dd[:, cols] * scale
+    store(dd, d_out)
+    for b, slots in ((6, [gi.at[i] for i in range(8, ICI)]), (7, [gm.at[i % RING] for i in range(8, ICI)])):
+        for c, a in enumerate(slots):
+            part = (1.0 - EMA_DECAY) * dot(gt[...], a[...], NN)
+            for j in range(2):
+                cols = pl.ds((c + 4 * j) * CW, CW)
+                rn[b, :, cols] = EMA_DECAY * rn[b, :, cols] + part[:, j * CW:(j + 1) * CW]
+        store(rn.at[b], r_out.at[:, columns(b, 0, N)])
+    halves = [gi.at[ICI - 1], gm.at[(ICI - 1) % RING]]
+    for n in range(N // TW):
+        cols = pl.ds(n * TW, TW)
+        part = sum(dot(a[...], a[cols, :], NT) for a in halves)
+        ln[:, cols] = ln[:, cols] + (1.0 - EMA_DECAY) * part
+    store(ln, l_out)
     for c in stores:
         c.wait()
 
@@ -356,14 +373,12 @@
         mids = pl.pallas_call(
             gather_kernel,
             name='gather_compute',
-            out_shape=(pltpu.VMEM((NDEV, N, N), F32), pltpu.VMEM((N, N), F32), pltpu.VMEM((N, N), F32), pltpu.VMEM((N, N), F32), pltpu.VMEM((8, CW), F32)),
+            out_shape=(pltpu.VMEM((NDEV, N, N), F32), pltpu.VMEM((N, N), F32), pltpu.VMEM((N, N), F32), pltpu.VMEM((N, N), F32), pltpu.VMEM((8, CW), F32),
+                       pltpu.VMEM((ICI, N, TW), BF16), pltpu.VMEM((RING, N, TW), BF16), pltpu.VMEM((N, N), BF16)),
             in_specs=[hbm] * 6,
-            out_specs=(vmem,) * 5,
+            out_specs=(vmem,) * 8,
             scratch_shapes=[
                 pltpu.VMEM((4, N, GW), BF16),
-                pltpu.VMEM((ICI, N, TW), BF16),
-                pltpu.VMEM((RING, N, TW), BF16),
-                pltpu.VMEM((N, N), BF16),
                 pltpu.VMEM((2, N, GW), BF16),
                 pltpu.VMEM((2, 8, CW), F32),
                 pltpu.VMEM((NDEV - 1, 2, 8, CW), F32),
@@ -374,14 +389,16 @@
             compiler_params=pltpu.CompilerParams(collective_id=0, has_side_effects=True, vmem_limit_bytes=VM1),
             cost_estimate=pl.CostEstimate(flops=46 * 2**30, bytes_accessed=60 * 2**20, transcendentals=2**20),
         )(grad_loc, left_stat, right_loc, left_root, root_loc, moment_loc)
-        left_new, right_new, direction, moment_new = pl.pallas_call(
+        left_new, right_new, direction, moment_new, _, _, _ = pl.pallas_call(
             write_kernel,
             name='write_results',
             out_shape=(jax.ShapeDtypeStruct((N, N), F32), jax.ShapeDtypeStruct((N, NDEV * N), F32),
-                       jax.ShapeDtypeStruct((N, N), F32), jax.ShapeDtypeStruct((N, N), F32)),
-            in_specs=[vmem] * 5,
-            out_specs=(hbm,) * 4,
-            scratch_shapes=[pltpu.VMEM((N, N), F32), dma((16,))],
+                       jax.ShapeDtypeStruct((N, N), F32), jax.ShapeDtypeStruct((N, N), F32),
+                       pltpu.VMEM((NDEV, N, N), F32), pltpu.VMEM((N, N), F32), pltpu.VMEM((N, N), F32)),
+            in_specs=[vmem] * 8,
+            out_specs=(hbm,) * 4 + (vmem,) * 3,
+            input_output_aliases={0: 4, 1: 5, 2: 6},
+            scratch_shapes=[dma((11,))],
             compiler_params=pltpu.CompilerParams(vmem_limit_bytes=VM2),
         )(*(pltpu.with_memory_space_constraint(t, pltpu.VMEM) for t in mids))
         return left_new, right_new, direction, moment_new
@@ -390,5 +407,5 @@
                          out_specs=(rep_spec, row_spec, col_spec, col_spec), check_vma=False)
 
 
-VM1 = 19 * 2**20
+VM1 = 9 * 2**20
 VM2 = VM1

time: 105 us -> 99.2 us (0.945)
  Pallas kernels: 104 us -> 98.3 us
    pallas_call x1, Pallas kernels: 89.2 us -> 83.4 us  [local_step(): pl.pallas_call(gather_kernel, name='gather_compute', out_shape=(pltpu.VME...]
where the time goes in v5:
time: 99.2 us; the launch traced here: 99.1 us
  Pallas kernels  98.3 us (99%)
    pallas_call x1, Pallas kernels, local_step(): pl.pallas_call(gather_kernel, name='gather_compute', out_shape=(pltpu.VME...  83.4 us
    pallas_call x1, Pallas kernels, local_step(): pl.pallas_call(write_kernel, name='write_results', out_shape=(jax.ShapeDt...  14.9 us

profile of v5, /device:TPU:0, one launch (start us, length us, event | category | flops | bytes accessed | tf_op | source)
XLA Modules:
  0.0 99.1 jit_solution(6762386820561836174)
XLA Ops:
  0.6 83.4 %gather_compute.1 = (f32[8,1024,1024]{2,1,0:T(8,128)S(1)}, f32[1024,1024]{1,0:T(8,128)S(1)}, f32[1024,1024]{1,0:T(8,128)S(1)}, f32[1024,1024]{1,0:T(8,128)S(1)},...) custom-call(bf16[1024,1024]{1,0:T(8,128)(2,1)} %g_hbm.1, ...), custom_call_target="tpu_custom_call" | custom-call | flops 49392123904 | bytes 62914560 | tf_op jit(solution)/shard_map/gather_compute/pallas_call | solution.py:373
  84.1 14.9 %write_results.1 = (f32[1024,1024]{1,0:T(8,128)}, f32[1024,8192]{1,0:T(8,128)}, f32[1024,1024]{1,0:T(8,128)}, f32[1024,1024]{1,0:T(8,128)}, f32[8,1024,1024]{2,1...) custom-call(f32[8,1024,1024]{2,1,0:T(8,128)S(1)} %get-tuple-element., ...), custom_call_target="tpu_custom_call", output_to_operand_aliasing={{4}: (0, {}), {5}: (1, {}), {6}: (2, {})} | custom-call | tf_op jit(solution)/shard_map/write_results/pallas_call | solution.py:392

commit v6 on v5

--- a/solution.py
+++ b/solution.py
@@ -73,12 +73,9 @@
     barrier = pltpu.get_barrier_semaphore()
     for k in range(1, NDEV):
         pl.semaphore_signal(barrier, inc=1, device_id={'tensor': lax.rem(me + k, NDEV)})
-    v_load.start()
     for c in rr_loads(local_pieces(0), 0):
         c.start()
     r_loads[0].start()
-    l_load.start()
-    r_loads[1].start()
     for c in own_loads:
         c.wait()
     pl.semaphore_wait(barrier, NDEV - 1)
@@ -102,6 +99,21 @@
     def send_forward(j):
         x_copy(8 + j, gi.at[j, :, lanes(1)]).start()
         y_copy(8 + j, gi.at[j, :, lanes(0)]).start()
+
+    pair = pl.ds(ICI - 2, 2)
+    row_half = [pl.ds(h * GW, GW) for h in range(2)]
+
+    def x_pair(h):
+        return pltpu.make_async_remote_copy(gi.at[pl.ds(2, 2), row_half[h], lanes(1)], gi.at[pair, row_half[h], lanes(0)],
+                                            x_s.at[ICI - 2 + h], x_r.at[ICI - 2 + h], device_id={'tensor': xnb})
+
+    def y_pair(h):
+        return pltpu.make_async_remote_copy(gi.at[pl.ds(2, 2), row_half[h], lanes(0)], gi.at[pair, row_half[h], lanes(1)],
+                                            y_s.at[ICI - 2 + h], y_r.at[ICI - 2 + h], device_id={'tensor': ynb})
+
+    def mate_pair(h):
+        return pltpu.make_async_remote_copy(gi.at[pair, row_half[h]], gm.at[pl.ds(RING - 2, 2), row_half[h]],
+                                            p_s.at[ICI - 2 + h], p_r.at[ICI - 2 + h], device_id={'tensor': mate})
 
     def mate_copy(i):
         return pltpu.make_async_remote_copy(gi.at[i], gm.at[i % RING], p_s.at[i], p_r.at[i], device_id={'tensor': mate})
@@ -110,28 +122,14 @@
         send_own(n)
     for h in range(2):
         own_send(h).start()
-    for c in r_loads[2:]:
-        c.start()
-
-    v_load.wait()
-
-    def adam(k, total):
-        rows = pl.ds(pl.multiple_of(k * 64, 64), 64)
-        for h in range(2):
-            grad = gl[h, rows, :].astype(F32)
-            moment = EMA_DECAY * vn[rows, lanes(h, GW)] + (1.0 - EMA_DECAY) * grad * grad
-            a = grad / (jnp.sqrt(moment) + ADAM_EPS)
-            vn[rows, lanes(h, GW)] = moment
-            dd[rows, lanes(h, GW)] = jnp.zeros((64, GW), F32)
-            total = total + jnp.sum(a * a, axis=0, keepdims=True)
-        return total
-
-    adam_sum = jnp.sum(lax.fori_loop(0, N // 64, adam, jnp.zeros((1, GW), F32)))
+    l_load.start()
+    r_loads[1].start()
 
     def transpose(k, _):
         rows = pl.ds(pl.multiple_of(k * CW, CW), CW)
         for h in range(2):
             gt[lanes(h, GW), rows] = gl[h, rows, :].T
+        dd[rows, :] = jnp.zeros((CW, N), F32)
         return 0
 
     lax.fori_loop(0, N // CW, transpose, 0)
@@ -177,14 +175,25 @@
 
         mate_copy(i).start()
 
+    def arrive_pair(h):
+        x_pair(h).wait_recv()
+        y_pair(h).wait_recv()
+        mate_pair(h).start()
+
     def issue(i):
         @pl.when(i < 8 - EARLY)
         def _():
             send_own(i + EARLY)
 
-        @pl.when((i >= 8 - EARLY) & (i < ICI - EARLY))
+        @pl.when((i >= 8 - EARLY) & (i < ICI - 2 - EARLY))
         def _():
             send_forward(i + EARLY - 8)
+
+        for h in range(2):
+            @pl.when(i == ICI - 2 - EARLY + h)
+            def _():
+                x_pair(h).start()
+                y_pair(h).start()
 
     def local_step(g, _):
         slot = g % 2
@@ -205,9 +214,16 @@
         def _():
             own_send(g - 2).wait()
 
+        @pl.when(g == 1)
+        def _():
+            for c in r_loads[2:4]:
+                c.start()
+
         @pl.when(g == 2)
         def _():
             r_loads[1].wait()
+            for c in r_loads[4:6]:
+                c.start()
 
         for c in rr_loads(where, slot):
             c.wait()
@@ -218,7 +234,7 @@
         def _():
             arrive(0)
             issue(0)
-            for c in r_loads[2:]:
+            for c in r_loads[2:6]:
                 c.wait()
 
         r_part(halves[1], where[2:])
@@ -226,6 +242,8 @@
         return 0
 
     lax.fori_loop(0, 4, local_step, 0)
+    v_load.start()
+    r_loads[6].start()
 
     lr_loads = [pltpu.make_async_copy(lr_hbm.at[:, h * GW:(h + 1) * GW], gl.at[h], lr_sem.at[h]) for h in range(2)]
 
@@ -250,49 +268,84 @@
 
     lax.fori_loop(0, 8, step, 0)
 
-    def late_step(i, _):
-        slot = i % 2
+    def late_step(i, slot):
         for c in rr_loads(pieces(5 + i), 1 - slot):
             c.start()
-
-        @pl.when(i == 9)
-        def _():
-            for n in range(8):
-                x_copy(n, own_chunk((n + 4) % 8)).wait_send()
-                y_copy(n, own_chunk(n)).wait_send()
-            for c in lr_loads:
-                c.start()
-
         mate_copy(i).wait_recv()
         for c in rr_loads(pieces(4 + i), slot):
             c.wait()
         x_part([gi.at[i], gm.at[i % RING]], slot)
-        arrive(i + 1)
-        l_part([gi.at[i], gm.at[i % RING]], half)
-        return 0
-
-    last = ICI - 1
-    lax.fori_loop(8, last, late_step, 0)
+
+    late_step(8, 0)
+
+    v_load.wait()
+
+    def adam(k, total):
+        rows = pl.ds(pl.multiple_of(k * 64, 64), 64)
+        for h in range(2):
+            grad = gl[h, rows, :].astype(F32)
+            moment = EMA_DECAY * vn[rows, lanes(h, GW)] + (1.0 - EMA_DECAY) * grad * grad
+            a = grad / (jnp.sqrt(moment) + ADAM_EPS)
+            vn[rows, lanes(h, GW)] = moment
+            total = total + jnp.sum(a * a, axis=0, keepdims=True)
+        return total
+
+    adam_sum = jnp.sum(lax.fori_loop(0, N // 64, adam, jnp.zeros((1, GW), F32)))
+
+    arrive(jnp.int32(9))
+    l_part([gi.at[8], gm.at[0]], half)
+    for n in range(8):
+        x_copy(n, own_chunk((n + 4) % 8)).wait_send()
+        y_copy(n, own_chunk(n)).wait_send()
+    for c in lr_loads:
+        c.start()
+    late_step(9, 1)
+    for c in rr_loads(pieces(15), 1):
+        c.start()
+    pl.semaphore_wait(credit, 2)
+    arrive_pair(0)
+    l_part([gi.at[9], gm.at[1]], half)
 
     l_send = pltpu.make_async_remote_copy(ln.at[half, :], ln.at[half, :], own_s.at[2], own_r.at[2], device_id={'tensor': mate})
     l_send.start()
-    slot = last % 2
-    for c in rr_loads(pieces(4 + last), slot):
-        c.wait()
-    x_part([gi.at[last]], slot)
+
+    for slot in range(2):
+        for c in rr_loads(pieces(14 + slot), slot):
+            c.wait()
     for c in lr_loads:
         c.wait()
-    mate_copy(last).wait_recv()
+    share = rn.at[NDEV - 1]
+
+    def x_rows(rows, mine_too, mates_too, done):
+        for n in range(N // TW):
+            cols = lanes(n, TW)
+            value = dd[rows, cols]
+            part = None
+            for k in range(2):
+                for take, a, at in ((mine_too, gi.at[ICI - 2 + k], 0), (mates_too, gm.at[RING - 2 + k], 1)):
+                    if take:
+                        term = dot(a[rows, :], rr[k, cols, lanes(at, TW)], NT)
+                        part = term if part is None else part + term
+            if done:
+                gl[2 + n // 2, rows, lanes(n % 2, TW)] = (value + part).astype(BF16)
+            else:
+                dd[rows, cols] = value + part
+
+    mate_pair(0).wait_recv()
+    x_rows(row_half[0], True, True, True)
+    for n in range(N // TW):
+        share[:, lanes(n, TW)] = dot(gl[0], gl[2 + n // 2, row_half[0], lanes(n % 2, TW)], NN)
+    arrive_pair(1)
+    x_rows(row_half[1], True, False, False)
+    mate_pair(1).wait_recv()
+    x_rows(row_half[1], False, True, True)
+    total = jnp.zeros((1, TW), F32)
     for n in range(N // TW):
         cols = lanes(n, TW)
-        part = dot(gm[last % RING], rr[slot, cols, lanes(1, TW)], NT)
-        gl[2 + n // 2, :, lanes(n % 2, TW)] = (dd[:, cols] + part).astype(BF16)
-    total = jnp.zeros((1, TW), F32)
-    for n in range(N // TW):
-        src = lanes(n % 2, TW)
-        part = dot(gl[0], gl[2 + n // 2, 0:GW, src], NN) + dot(gl[1], gl[2 + n // 2, GW:N, src], NN)
-        dd[:, lanes(n, TW)] = part
+        part = share[:, cols] + dot(gl[1], gl[2 + n // 2, row_half[1], lanes(n % 2, TW)], NN)
+        dd[:, cols] = part
         total = total + jnp.sum(part * part, axis=0, keepdims=True)
+    r_loads[NDEV - 1].start()
     mine[0] = jnp.full((8, CW), adam_sum, F32)
     mine[1] = jnp.full((8, CW), jnp.sum(total), F32)
 
@@ -314,11 +367,16 @@
 
     for k in range(1, NDEV):
         norm_copy(NDEV - 1 - k, NDEV - 1 - k, lax.rem(me + k, NDEV)).wait_send()
-    for j in range(4):
+    for j in range(2):
         x_copy(8 + j, gi.at[j, :, lanes(1)]).wait_send()
         y_copy(8 + j, gi.at[j, :, lanes(0)]).wait_send()
-    for i in range(ICI):
+        x_pair(j).wait_send()
+        y_pair(j).wait_send()
+        mate_pair(j).wait_send()
+    for i in range(ICI - 2):
         mate_copy(i).wait_send()
+    for c in r_loads[6:]:
+        c.wait()
 
 
 def write_kernel(rn_in, dd_in, ln_in, vn, ratio, gi, gm, gt, l_out, r_out, d_out, v_out, rn, dd, ln, sem):
@@ -337,25 +395,25 @@
         return pl.ds(pl.multiple_of(dev * N + c * CW, CW), w)
 
     for b in range(6):
-        store(rn.at[b], r_out.at[:, columns(b, 0, N)])
+        store(rn_in.at[b], r_out.at[:, columns(b, 0, N)])
     store(vn, v_out)
     scale = ratio[0:1, 0:1]
     for n in range(N // TW):
         cols = pl.ds(n * TW, TW)
-        dd[:, cols] = dd[:, cols] * scale
+        dd[:, cols] = dd_in[:, cols] * scale
     store(dd, d_out)
     for b, slots in ((6, [gi.at[i] for i in range(8, ICI)]), (7, [gm.at[i % RING] for i in range(8, ICI)])):
         for c, a in enumerate(slots):
             part = (1.0 - EMA_DECAY) * dot(gt[...], a[...], NN)
             for j in range(2):
                 cols = pl.ds((c + 4 * j) * CW, CW)
-                rn[b, :, cols] = EMA_DECAY * rn[b, :, cols] + part[:, j * CW:(j + 1) * CW]
+                rn[b, :, cols] = EMA_DECAY * rn_in[b, :, cols] + part[:, j * CW:(j + 1) * CW]
         store(rn.at[b], r_out.at[:, columns(b, 0, N)])
-    halves = [gi.at[ICI - 1], gm.at[(ICI - 1) % RING]]
+    halves = [gi.at[ICI - 2], gi.at[ICI - 1], gm.at[RING - 2], gm.at[RING - 1]]
     for n in range(N // TW):
         cols = pl.ds(n * TW, TW)
         part = sum(dot(a[...], a[cols, :], NT) for a in halves)
-        ln[:, cols] = ln[:, cols] + (1.0 - EMA_DECAY) * part
+        ln[:, cols] = ln_in[:, cols] + (1.0 - EMA_DECAY) * part
     store(ln, l_out)
     for c in stores:
         c.wait()
@@ -407,5 +465,5 @@
                          out_specs=(rep_spec, row_spec, col_spec, col_spec), check_vma=False)
 
 
-VM1 = 9 * 2**20
+VM1 = 79 * 2**17
 VM2 = VM1

time: 99.2 us -> 96.9 us (0.977)
  Pallas kernels: 98.3 us -> 96 us
    pallas_call x1, Pallas kernels: 83.4 us -> 81.2 us  [local_step(): pl.pallas_call(gather_kernel, name='gather_compute', out_shape=(pltpu.VME...]
where the time goes in v6:
time: 96.9 us; the launch traced here: 96.8 us
  Pallas kernels  96 us (99%)
    pallas_call x1, Pallas kernels, local_step(): pl.pallas_call(gather_kernel, name='gather_compute', out_shape=(pltpu.VME...  81.2 us
    pallas_call x1, Pallas kernels, local_step(): pl.pallas_call(write_kernel, name='write_results', out_shape=(jax.ShapeDt...  14.9 us

profile of v6, /device:TPU:0, one launch (start us, length us, event | category | flops | bytes accessed | tf_op | source)
XLA Modules:
  0.0 96.8 jit_solution(9629364851818146284)
XLA Ops:
  0.6 81.2 %gather_compute.1 = (f32[8,1024,1024]{2,1,0:T(8,128)S(1)}, f32[1024,1024]{1,0:T(8,128)S(1)}, f32[1024,1024]{1,0:T(8,128)S(1)}, f32[1024,1024]{1,0:T(8,128)S(1)},...) custom-call(bf16[1024,1024]{1,0:T(8,128)(2,1)} %g_hbm.1, ...), custom_call_target="tpu_custom_call" | custom-call | flops 49392123904 | bytes 62914560 | tf_op jit(solution)/shard_map/gather_compute/pallas_call | solution.py:431
  81.8 14.9 %write_results.1 = (f32[1024,1024]{1,0:T(8,128)}, f32[1024,8192]{1,0:T(8,128)}, f32[1024,1024]{1,0:T(8,128)}, f32[1024,1024]{1,0:T(8,128)}, f32[8,1024,1024]{2,1...) custom-call(f32[8,1024,1024]{2,1,0:T(8,128)S(1)} %get-tuple-element., ...), custom_call_target="tpu_custom_call", output_to_operand_aliasing={{4}: (0, {}), {5}: (1, {}), {6}: (2, {})} | custom-call | tf_op jit(solution)/shard_map/write_results/pallas_call | solution.py:450

commit v7 on v6

--- a/solution.py
+++ b/solution.py
@@ -115,6 +115,10 @@
         return pltpu.make_async_remote_copy(gi.at[pair, row_half[h]], gm.at[pl.ds(RING - 2, 2), row_half[h]],
                                             p_s.at[ICI - 2 + h], p_r.at[ICI - 2 + h], device_id={'tensor': mate})
 
+    def mate_low(k):
+        return pltpu.make_async_remote_copy(gi.at[ICI - 2 + k, row_half[1]], gm.at[RING - 2 + k, row_half[1]],
+                                            p_s.at[ICI - 1 + k], p_r.at[ICI - 1 + k], device_id={'tensor': mate})
+
     def mate_copy(i):
         return pltpu.make_async_remote_copy(gi.at[i], gm.at[i % RING], p_s.at[i], p_r.at[i], device_id={'tensor': mate})
 
@@ -178,7 +182,11 @@
     def arrive_pair(h):
         x_pair(h).wait_recv()
         y_pair(h).wait_recv()
-        mate_pair(h).start()
+        if h == 0:
+            mate_pair(0).start()
+        else:
+            for k in range(2):
+                mate_low(k).start()
 
     def issue(i):
         @pl.when(i < 8 - EARLY)
@@ -316,12 +324,12 @@
         c.wait()
     share = rn.at[NDEV - 1]
 
-    def x_rows(rows, mine_too, mates_too, done):
+    def x_rows(rows, mine_too, mates_too, done, chunks=(0, 1)):
         for n in range(N // TW):
             cols = lanes(n, TW)
             value = dd[rows, cols]
             part = None
-            for k in range(2):
+            for k in chunks:
                 for take, a, at in ((mine_too, gi.at[ICI - 2 + k], 0), (mates_too, gm.at[RING - 2 + k], 1)):
                     if take:
                         term = dot(a[rows, :], rr[k, cols, lanes(at, TW)], NT)
@@ -337,15 +345,16 @@
         share[:, lanes(n, TW)] = dot(gl[0], gl[2 + n // 2, row_half[0], lanes(n % 2, TW)], NN)
     arrive_pair(1)
     x_rows(row_half[1], True, False, False)
-    mate_pair(1).wait_recv()
-    x_rows(row_half[1], False, True, True)
+    mate_low(0).wait_recv()
+    x_rows(row_half[1], False, True, False, (0,))
+    mate_low(1).wait_recv()
+    x_rows(row_half[1], False, True, True, (1,))
     total = jnp.zeros((1, TW), F32)
     for n in range(N // TW):
         cols = lanes(n, TW)
         part = share[:, cols] + dot(gl[1], gl[2 + n // 2, row_half[1], lanes(n % 2, TW)], NN)
         dd[:, cols] = part
         total = total + jnp.sum(part * part, axis=0, keepdims=True)
-    r_loads[NDEV - 1].start()
     mine[0] = jnp.full((8, CW), adam_sum, F32)
     mine[1] = jnp.full((8, CW), jnp.sum(total), F32)
 
@@ -354,6 +363,7 @@
 
     for k in range(1, NDEV):
         norm_copy(NDEV - 1 - k, NDEV - 1 - k, lax.rem(me + k, NDEV)).start()
+    r_loads[NDEV - 1].start()
     l_send.wait()
     for k in range(1, NDEV):
         norm_copy(k - 1, k - 1, lax.rem(me + k, NDEV)).wait_recv()
@@ -372,7 +382,8 @@
         y_copy(8 + j, gi.at[j, :, lanes(0)]).wait_send()
         x_pair(j).wait_send()
         y_pair(j).wait_send()
-        mate_pair(j).wait_send()
+        mate_low(j).wait_send()
+    mate_pair(0).wait_send()
     for i in range(ICI - 2):
         mate_copy(i).wait_send()
     for c in r_loads[6:]:
@@ -442,7 +453,7 @@
                 pltpu.VMEM((NDEV - 1, 2, 8, CW), F32),
                 dma((4,)), dma((8,)), dma((2, 4)), dma((2,)),
                 dma((3,)), dma((3,)), dma((ICI,)), dma((ICI,)), dma((ICI,)), dma((ICI,)),
-                dma((ICI,)), dma((ICI,)), dma((NDEV - 1,)), dma((NDEV - 1,)), pltpu.SemaphoreType.REGULAR,
+                dma((ICI + 1,)), dma((ICI + 1,)), dma((NDEV - 1,)), dma((NDEV - 1,)), pltpu.SemaphoreType.REGULAR,
             ],
             compiler_params=pltpu.CompilerParams(collective_id=0, has_side_effects=True, vmem_limit_bytes=VM1),
             cost_estimate=pl.CostEstimate(flops=46 * 2**30, bytes_accessed=60 * 2**20, transcendentals=2**20),

time: 96.9 us -> 96.7 us (level)
  no operation moved by 1% of the time
where the time goes in v7:
time: 96.7 us; the launch traced here: 96.6 us
  Pallas kernels  95.8 us (99%)
    pallas_call x1, Pallas kernels, local_step(): pl.pallas_call(gather_kernel, name='gather_compute', out_shape=(pltpu.VME...  80.9 us
    pallas_call x1, Pallas kernels, local_step(): pl.pallas_call(write_kernel, name='write_results', out_shape=(jax.ShapeDt...  14.9 us

profile of v7, /device:TPU:0, one launch (start us, length us, event | category | flops | bytes accessed | tf_op | source)
XLA Modules:
  0.0 96.6 jit_solution(8465964804197749089)
XLA Ops:
  0.6 80.9 %gather_compute.1 = (f32[8,1024,1024]{2,1,0:T(8,128)S(1)}, f32[1024,1024]{1,0:T(8,128)S(1)}, f32[1024,1024]{1,0:T(8,128)S(1)}, f32[1024,1024]{1,0:T(8,128)S(1)},...) custom-call(bf16[1024,1024]{1,0:T(8,128)(2,1)} %g_hbm.1, ...), custom_call_target="tpu_custom_call" | custom-call | flops 49392123904 | bytes 62914560 | tf_op jit(solution)/shard_map/gather_compute/pallas_call | solution.py:442
  81.5 14.9 %write_results.1 = (f32[1024,1024]{1,0:T(8,128)}, f32[1024,8192]{1,0:T(8,128)}, f32[1024,1024]{1,0:T(8,128)}, f32[1024,1024]{1,0:T(8,128)}, f32[8,1024,1024]{2,1...) custom-call(f32[8,1024,1024]{2,1,0:T(8,128)S(1)} %get-tuple-element., ...), custom_call_target="tpu_custom_call", output_to_operand_aliasing={{4}: (0, {}), {5}: (1, {}), {6}: (2, {})} | custom-call | tf_op jit(solution)/shard_map/write_results/pallas_call | solution.py:461
